TPU v7x, 32 devices: a whole 2x2x4 slice. The times are simulated.
32 devices in a mesh: row: 8 (over z, y), col: 4 (over x, core).
Axes of the slice: x: 2, y: 2, z: 4, core: 2. Of those that a mesh axis runs over, the one named last changes fastest.
Arguments:
- layer_input: bfloat16 [2048, 8192], P('row'), may hold values from -7 to 7
- gain: float32 [8192], replicated, may hold values from 0.5 to 6
- d_query: bfloat16 [2048, 4096], P('row', 'col'), may hold values from -6 to 6
- d_keyval: bfloat16 [2048, 2048], P('row', 'col'), may hold values from -6 to 6
- w_query: bfloat16 [8192, 4096], P('row', 'col'), may hold values from -0.0625 to 0.0625
- w_keyval: bfloat16 [8192, 2048], P('row', 'col'), may hold values from -1 to 1
- d_resid: bfloat16 [2048, 8192], P('row', 'col'), may hold values from -6 to 6
Outputs:
- d_input: bfloat16 [2048, 8192], P('row', 'col')
- grad_wq: bfloat16 [8192, 4096], P('row', 'col')
- grad_wkv: bfloat16 [8192, 2048], P('row', 'col')
- grad_gain: float32 [8192], P('col')
- grad_square_sum: float32 [], replicated
All inputs are finite; a program needn't handle non-finite values.
Results may differ from a plain program's by a relative error of at most 0.023.
Values may be sent and summed in bfloat16 or wider, within the bound.
A program may use at most 128 MiB of HBM per device.

v0:
```python
import functools
import math

import jax
import jax.numpy as jnp
from jax import lax
from jax.experimental import pallas as pl
from jax.experimental.pallas import tpu as pltpu
from jax.sharding import PartitionSpec as P

epsilon = 1e-05
MESH = pl.DeviceIdType.MESH
PIECES = 2


def ring_order(place, n):
    return jnp.where(place < n // 2, 2 * place, 2 * (n - 1 - place) + 1)


def ring_place(index, n):
    half = index // 2
    return jnp.where(index % 2 == 0, half, n - 1 - half)


def greet(row, col, n_row, n_col):
    barrier = pltpu.get_barrier_semaphore()
    for k in range(1, n_row):
        pl.semaphore_signal(
            barrier, inc=1, device_id=((row + k) % n_row, col), device_id_type=MESH
        )
    for k in range(1, n_col):
        pl.semaphore_signal(
            barrier, inc=1, device_id=(row, (col + k) % n_col), device_id_type=MESH
        )
    pl.semaphore_wait(barrier, n_row + n_col - 2)


def gather_kernel(
    n_row, n_col, cot, normed, all_cot, columns,
    own_sem, ring_send, ring_recv, swap_send, swap_recv, share_send, share_recv,
):
    row, col = lax.axis_index("row"), lax.axis_index("col")
    tokens = cot.shape[0]
    width = columns.shape[2]
    part = tokens // n_col
    piece = tokens // (2 * PIECES)
    place = ring_place(row, n_row)
    ahead = ring_order((place + 1) % n_row, n_row)
    behind = ring_order((place + n_row - 1) % n_row, n_row)
    greet(row, col, n_row, n_col)

    own_rows = pl.ds(pl.multiple_of(col * part, part), part)

    def ring_copy(step, way, q):
        if way == 0:
            source, target = ring_order((place + n_row - step) % n_row, n_row), ahead
        else:
            source, target = ring_order((place + step) % n_row, n_row), behind
        rows = pl.ds((way * PIECES + q) * piece, piece)
        return pltpu.make_async_remote_copy(
            src_ref=cot.at[rows] if step == 0 else all_cot.at[source, rows],
            dst_ref=all_cot.at[source, rows],
            send_sem=ring_send.at[step, way, q],
            recv_sem=ring_recv.at[step, way, q],
            device_id=(target, col),
            device_id_type=MESH,
        )

    def swap_copy(k):
        target = ring_order((place + k) % n_row, n_row)
        return pltpu.make_async_remote_copy(
            src_ref=normed.at[own_rows, pl.ds(pl.multiple_of(target * width, width), width)],
            dst_ref=columns.at[row, own_rows],
            send_sem=swap_send.at[k],
            recv_sem=swap_recv.at[k],
            device_id=(target, col),
            device_id_type=MESH,
        )

    own_columns = pl.ds(pl.multiple_of(row * width, width), width)

    def share_copy(k, j):
        source = ring_order((place + n_row - k) % n_row, n_row)
        return pltpu.make_async_remote_copy(
            src_ref=columns.at[source, own_rows],
            dst_ref=columns.at[source, own_rows],
            send_sem=share_send.at[k, j],
            recv_sem=share_recv.at[k, j],
            device_id=(row, (col + j) % n_col),
            device_id_type=MESH,
        )

    keep_cot = pltpu.make_async_copy(cot, all_cot.at[row], own_sem.at[0])
    keep_normed = pltpu.make_async_copy(
        normed.at[:, own_columns], columns.at[row], own_sem.at[1]
    )
    rings = {}
    swaps = {}
    shares = []
    for step in range(n_row):
        for q in range(PIECES):
            for way in range(2):
                if step > 0:
                    rings[step - 1, way, q].wait_recv()
                if step < n_row - 1:
                    rings[step, way, q] = ring_copy(step, way, q)
                    rings[step, way, q].start()
        if step == 0:
            keep_cot.start()
            keep_normed.start()
        if step < n_row - 1:
            swaps[step + 1] = swap_copy(step + 1)
            swaps[step + 1].start()
        if step > 0:
            swaps[step].wait_recv()
            for j in range(1, n_col):
                copy = share_copy(step, j)
                copy.start()
                shares.append(copy)
    keep_cot.wait()
    keep_normed.wait()
    for copy in list(rings.values()) + list(swaps.values()):
        copy.wait_send()
    for copy in shares:
        copy.wait()


def gather(cot, normed, n_row, n_col):
    tokens, cot_width = cot.shape
    width = normed.shape[1] // n_row
    dma = pltpu.SemaphoreType.DMA
    return pl.pallas_call(
        functools.partial(gather_kernel, n_row, n_col),
        out_shape=(
            jax.ShapeDtypeStruct((n_row, tokens, cot_width), cot.dtype),
            jax.ShapeDtypeStruct((n_row, tokens, width), normed.dtype),
        ),
        in_specs=[pl.BlockSpec(memory_space=pltpu.VMEM)] * 2,
        out_specs=[pl.BlockSpec(memory_space=pl.ANY)] * 2,
        scratch_shapes=[
            dma((2,)),
            dma((n_row, 2, PIECES)),
            dma((n_row, 2, PIECES)),
            dma((n_row,)),
            dma((n_row,)),
            dma((n_row, n_col)),
            dma((n_row, n_col)),
        ],
        compiler_params=pltpu.CompilerParams(collective_id=0, has_side_effects=True),
        name="gather",
    )(cot, normed)


def sums_kernel(
    n_row, n_col, dots, gains, dots_out, gains_out,
    dots_in, gains_in, dots_send, dots_recv, gains_send, gains_recv,
):
    row, col = lax.axis_index("row"), lax.axis_index("col")
    greet(row, col, n_row, n_col)
    copies = []
    for k in range(1, n_col):
        copies.append(
            pltpu.make_async_remote_copy(
                src_ref=dots,
                dst_ref=dots_in.at[col],
                send_sem=dots_send.at[k],
                recv_sem=dots_recv.at[k],
                device_id=(row, (col + k) % n_col),
                device_id_type=MESH,
            )
        )
    for k in range(1, n_row):
        copies.append(
            pltpu.make_async_remote_copy(
                src_ref=gains,
                dst_ref=gains_in.at[row],
                send_sem=gains_send.at[k],
                recv_sem=gains_recv.at[k],
                device_id=((row + k) % n_row, col),
                device_id_type=MESH,
            )
        )
    for copy in copies:
        copy.start()
    dots_in[col] = dots[...]
    gains_in[row] = gains[...]
    for copy in copies:
        copy.wait()
    dots_out[...] = jnp.sum(dots_in[...], axis=0)
    gains_out[...] = jnp.sum(gains_in[...], axis=0)


def sums(dots, gains, n_row, n_col):
    dma = pltpu.SemaphoreType.DMA
    return pl.pallas_call(
        functools.partial(sums_kernel, n_row, n_col),
        out_shape=(
            jax.ShapeDtypeStruct(dots.shape, dots.dtype),
            jax.ShapeDtypeStruct(gains.shape, gains.dtype),
        ),
        in_specs=[pl.BlockSpec(memory_space=pltpu.VMEM)] * 2,
        out_specs=[pl.BlockSpec(memory_space=pltpu.VMEM)] * 2,
        scratch_shapes=[
            pltpu.VMEM((n_col,) + dots.shape, dots.dtype),
            pltpu.VMEM((n_row,) + gains.shape, gains.dtype),
            dma((n_col,)),
            dma((n_col,)),
            dma((n_row,)),
            dma((n_row,)),
        ],
        compiler_params=pltpu.CompilerParams(collective_id=1, has_side_effects=True),
        name="sums",
    )(dots, gains)


def total_kernel(n_col, value, result, arrived, send_sem, recv_sem):
    row, col = lax.axis_index("row"), lax.axis_index("col")
    barrier = pltpu.get_barrier_semaphore()
    for k in range(1, n_col):
        pl.semaphore_signal(
            barrier, inc=1, device_id=(row, (col + k) % n_col), device_id_type=MESH
        )
    pl.semaphore_wait(barrier, n_col - 1)
    copies = [
        pltpu.make_async_remote_copy(
            src_ref=value,
            dst_ref=arrived.at[col],
            send_sem=send_sem.at[k],
            recv_sem=recv_sem.at[k],
            device_id=(row, (col + k) % n_col),
            device_id_type=MESH,
        )
        for k in range(1, n_col)
    ]
    for copy in copies:
        copy.start()
    arrived[col] = value[...]
    for copy in copies:
        copy.wait()
    result[...] = jnp.sum(arrived[...], axis=0)


def total(value, n_col):
    block = jnp.full((8, 128), value, jnp.float32)
    return pl.pallas_call(
        functools.partial(total_kernel, n_col),
        out_shape=jax.ShapeDtypeStruct(block.shape, block.dtype),
        in_specs=[pl.BlockSpec(memory_space=pltpu.VMEM)],
        out_specs=pl.BlockSpec(memory_space=pltpu.VMEM),
        scratch_shapes=[
            pltpu.VMEM((n_col,) + block.shape, block.dtype),
            pltpu.SemaphoreType.DMA((n_col,)),
            pltpu.SemaphoreType.DMA((n_col,)),
        ],
        compiler_params=pltpu.CompilerParams(collective_id=2, has_side_effects=True),
        name="total",
    )(block)[0, 0]


def local(layer_input, gain, d_query, d_keyval, w_query, w_keyval, d_resid):
    inputs = layer_input.astype(jnp.float32)
    inv_rms = lax.rsqrt(jnp.mean(inputs * inputs, axis=1, keepdims=True) + epsilon)
    normed = (inputs * inv_rms * gain).astype(jnp.bfloat16)
    model_width = inputs.shape[1]
    local_tokens = inputs.shape[0]
    tokens_all = local_tokens * lax.axis_size("row")
    scaling = 1.0 / math.sqrt(tokens_all)
    weight_scale = 1.0 / math.sqrt(local_tokens)
    contract_cols = (((1,), (1,)), ((), ()))
    query_cols = d_query.shape[1]
    cotangent = jnp.concatenate([d_query, d_keyval], axis=1)
    n_row, n_col = lax.axis_size("row"), lax.axis_size("col")
    all_cotangents, columns = gather(cotangent, normed, n_row, n_col)
    all_cotangents = all_cotangents.reshape(-1, cotangent.shape[1])
    columns = columns.reshape(all_cotangents.shape[0], -1)
    weights = jnp.concatenate([w_query, w_keyval], axis=1)
    partial_value = lax.dot_general(
        all_cotangents, weights, contract_cols, preferred_element_type=jnp.float32
    )
    reduced = lax.psum_scatter(
        partial_value.astype(jnp.bfloat16), "col", scatter_dimension=0, tiled=True
    )
    fold = n_row // n_col
    pieces = reduced.reshape(fold, local_tokens, reduced.shape[1])
    row, col = lax.axis_index("row"), lax.axis_index("col")
    arrived = []
    for shift in range(fold):
        pairs = [
            (r * n_col + c, (fold * c + (r + shift) % fold) * n_col + r // fold)
            for r in range(n_row)
            for c in range(n_col)
        ]
        piece = lax.dynamic_index_in_dim(pieces, (row + shift) % fold, 0, keepdims=False)
        arrived.append(lax.ppermute(piece, ("row", "col"), pairs))
    arrived = jnp.stack(arrived)
    feature_grad = jnp.concatenate(
        [
            lax.dynamic_index_in_dim(arrived, (row - j + fold) % fold, 0, keepdims=False)
            for j in range(fold)
        ],
        axis=1,
    ).astype(jnp.float32)
    slice_width = feature_grad.shape[1]
    col_start = lax.axis_index("col") * slice_width
    input_part = lax.dynamic_slice_in_dim(layer_input, col_start, slice_width, 1).astype(
        jnp.float32
    )
    gain_part = lax.dynamic_slice_in_dim(gain, col_start, slice_width, 0)
    weighted = gain_part * feature_grad
    summed = (
        lax.dot_general(
            columns, all_cotangents, (((0,), (0,)), ((), ())), preferred_element_type=jnp.float32
        )
        * weight_scale
    )
    grad_wq = summed[:, :query_cols].astype(jnp.bfloat16)
    grad_wkv = summed[:, query_cols:].astype(jnp.bfloat16)
    query_f = grad_wq.astype(jnp.float32)
    keyval_f = grad_wkv.astype(jnp.float32)
    tile_square = jnp.sum(query_f * query_f) + jnp.sum(keyval_f * keyval_f)
    gain_partial = jnp.sum(feature_grad * input_part * inv_rms, axis=0) * scaling
    dots, gains = sums(
        jnp.sum(weighted * input_part, axis=1).reshape(-1, 128),
        jnp.concatenate([gain_partial.reshape(-1, 128), jnp.full((8, 128), tile_square)]),
        n_row,
        n_col,
    )
    token_dot = dots.reshape(local_tokens, 1)
    grad_gain = gains[:-8].reshape(slice_width)
    d_input = (
        d_resid.astype(jnp.float32)
        + inv_rms * weighted
        - input_part * inv_rms**3 * token_dot / model_width
    ).astype(jnp.bfloat16)
    grand_total = total(gains[-1, 0] + jnp.sum(grad_gain * grad_gain), n_col)
    grad_square_sum = grand_total / jnp.float32(model_width)
    return (d_input, grad_wq, grad_wkv, grad_gain, grad_square_sum)


def solution(mesh):
    placed = (
        P("row", None),
        P(),
        P("row", "col"),
        P("row", "col"),
        P("row", "col"),
        P("row", "col"),
        P("row", "col"),
    )
    return jax.shard_map(
        local,
        mesh=mesh,
        in_specs=placed,
        out_specs=(P("row", "col"), P("row", "col"), P("row", "col"), P("col"), P()),
        check_vma=False,
    )
```

profile of v0, /device:TPU:0, one launch (start us, length us, event | category | flops | bytes accessed | tf_op | source)
XLA Modules:
  0.0 260.3 jit_solution(11702169825339784474)
XLA Ops:
  7.2 0.0 copy-start.3
  7.2 0.0 copy-start.2
  7.2 0.0 copy-start.4
  7.2 0.0 reduce-scatter.2.cloned.1.call-start
  7.2 0.0 copy-start
  7.3 3.3 %fusion = f32[256]{0:T(256)S(1)} fusion(bf16[256,8192]{1,0:T(8,128)(2,1)} %param.7), kind=kLoop, calls=%fused_computation.2 | loop fusion | flops 6291200 | bytes 4195328 | tf_op jit(solution)/shard_map/reduce_sum | solution.py:262
  10.5 0.0 copy-done.3
  10.5 0.0 copy-done.2
  10.5 0.9 pad_maximum_fusion.1.cot
  11.5 3.3 %fusion.2.normed = bf16[256,8192]{1,0:T(8,128)(2,1)} fusion(bf16[256,8192]{1,0:T(8,128)(2,1)S(1)} %copy-done, f32[8192]{0:T(1024)S(1)} %copy-done.4, f32[256]{0:T(256)S(1)} %get-tuple-element.26), kind=kLoop, calls=%fused_computation.4 | loop fusion | flops 8388608 | bytes 8422400 | tf_op jit(solution)/shard_map/convert_element_type | solution.py:263
  14.7 102.3 %gather.1 = (bf16[8,256,1536]{2,1,0:T(8,128)(2,1)}, bf16[8,256,1024]{2,1,0:T(8,128)(2,1)}) custom-call(bf16[256,1536]{1,0:T(8,128)(2,1)} %pad_maximum_fusion.1.cot, bf16[256,8192]{1,0:T(8,128)(2,1)} %fusion.2.normed), custom_call_target="tpu_custom_call" | custom-call | tf_op jit(solution)/shard_map/gather/pallas_call | solution.py:132
  117.1 11.1 %convolution_convert_fusion = bf16[2048,1024]{1,0:T(8,128)(2,1)} fusion(bf16[2048,1536]{1,0:T(8,128)(2,1)} %bitcast.30, bf16[1024,512]{1,0:T(8,128)(2,1)S(1)} %copy-done.6, bf16[1024,1024]{1,0:T(8,128)(2,1)S(1)} %copy-done.5), kind=kOutput, calls=%fused_computation.8 | convolution fusion | flops 6450839552 | bytes 13631488 | tf_op jit(solution)/shard_map/dot_general | solution.py:277
  128.2 0.0 reduce-scatter.2.cloned.1.call-update
  128.3 10.3 %fusion.3 = bf16[1024,1536]{1,0:T(8,128)(2,1)S(1)} fusion(bf16[8,256,1024]{2,1,0:T(8,128)(2,1)} %get-tuple-element.10, bf16[8,256,1536]{2,1,0:T(8,128)(2,1)} %get-tuple-element.9), kind=kOutput, calls=%fused_computation.6 | convolution fusion | flops 6445596672 | bytes 13631488 | tf_op jit(solution)/shard_map/dot_general | solution.py:311
  138.5 34.7 %reduce-scatter.2.cloned.1.call-done = bf16[512,1024]{1,0:T(8,128)(2,1)} async-done(((bf16[2048,1024]{1,0:T(8,128)(2,1)}), bf16[512,1024]{1,0:T(8,128)(2,1)}) %reduce-scatter.2.cloned.1.call-update) | async-done | bytes 1048592 | tf_op jit(solution)/shard_map/reduce_scatter | solution.py:280
  173.2 2.2 dynamic-slice_bitcast_fusion
  175.4 1.5 collective-permute-start.1
  176.9 5.4 %collective-permute-start = (bf16[256,1024]{1,0:T(8,128)(2,1)}, bf16[256,1024]{1,0:T(8,128)(2,1)}, u32[]{:S(2)}, u32[]{:S(2)}) collective-permute-start(bf16[256,1024]{1,0:T(8,128)(2,1)} %get-tuple-element.22), channel_id=1, source_target_pairs={{0,0},{1,8},{2,16},{3,24},{4,4},{5,12},{6,20},{7,28},{8,1},{9,9},{... | collective-permute-start | bytes 1572872 | tf_op jit(solution)/shard_map/ppermute | solution.py:294
  182.3 2.0 multiply_reduce_fusion.1
  184.3 2.9 %multiply_reduce_fusion = (f32[]{:T(128)}, bf16[1024,1024]{1,0:T(8,128)(2,1)}) fusion(bf16[1024,1536]{1,0:T(8,128)(2,1)S(1)} %fusion.3), kind=kLoop, calls=%fused_computation.7 | loop fusion | flops 3145727 | bytes 4194308 | tf_op jit(solution)/shard_map/reduce_sum | solution.py:320
  188.7 1.9 collective-permute-done.1
  190.6 0.0 collective-permute-done
  190.6 1.6 fusion.19
  192.1 2.4 fusion.15
  194.6 0.6 concatenate.15.gains
  195.2 41.3 %sums.1 = (f32[2,128]{1,0:T(2,128)}, f32[24,128]{1,0:T(8,128)}) custom-call(f32[2,128]{1,0:T(2,128)} %bitcast.28, f32[24,128]{1,0:T(8,128)} %concatenate.15.gains), custom_call_target="tpu_custom_call" | custom-call | tf_op jit(solution)/shard_map/sums/pallas_call | solution.py:195
  236.5 1.2 slice.20
  237.7 1.9 multiply_reduce_fusion.2
  240.9 0.6 broadcast_in_dim.2.value
  241.5 6.0 %total.1 = f32[8,128]{1,0:T(8,128)} custom-call(f32[8,128]{1,0:T(8,128)} %broadcast_in_dim.2.value), custom_call_target="tpu_custom_call" | custom-call | tf_op jit(solution)/shard_map/total/pallas_call | solution.py:245
  247.5 1.2 slice.21
  249.3 3.0 %fusion.10 = bf16[256,2048]{1,0:T(8,128)(2,1)} fusion(bf16[256,2048]{1,0:T(8,128)(2,1)S(1)} %copy-done.1, f32[256]{0:T(256)} %bitcast.29, f32[256]{0:T(256)S(1)} %get-tuple-element.25, f32[2048]{0:T(1024)S(1)} %dynamic_slice.19, f32[256]{0:T(256)S(1)} %get-tuple-element.26, bf16[256,8192]{1,0:T(8,128)(2,1)} %param.7, s32[]{:T(128)S(6)} %select_n.32, ...), kind=kLoop, calls=%fused_computation.19 | loop fusion | flops 7340032 | bytes 4205572 | tf_op jit(solution)/shard_map/convert_element_type | solution.py:334
  (11 shorter events, 0.0 us)
Async XLA Ops:
  7.2 3.4 %copy-start.3 = (bf16[256,512]{1,0:T(8,128)(2,1)S(1)}, bf16[256,512]{1,0:T(8,128)(2,1)}, u32[]{:S(2)}) copy-start(bf16[256,512]{1,0:T(8,128)(2,1)} %param.10) | copy-start | bytes 786436
  7.2 3.4 %copy-start.2 = (bf16[256,1024]{1,0:T(8,128)(2,1)S(1)}, bf16[256,1024]{1,0:T(8,128)(2,1)}, u32[]{:S(2)}) copy-start(bf16[256,1024]{1,0:T(8,128)(2,1)} %param.9) | copy-start | bytes 1572868
  7.2 4.3 %copy-start.4 = (f32[8192]{0:T(1024)S(1)}, f32[8192]{0:T(1024)}, u32[]{:S(2)}) copy-start(f32[8192]{0:T(1024)} %param.8) | copy-start | bytes 98308
  7.2 166.0 %reduce-scatter.2.cloned.1.call-start = ((), (), s32[]{:S(2)}) async-start(), calls=%async_computation.1 | async-start | bytes 5242880 | tf_op jit(solution)/shard_map/reduce_scatter | solution.py:280
  7.2 4.2 %copy-start = (bf16[256,8192]{1,0:T(8,128)(2,1)S(1)}, bf16[256,8192]{1,0:T(8,128)(2,1)}, u32[]{:S(2)}) copy-start(bf16[256,8192]{1,0:T(8,128)(2,1)} %param.7) | copy-start | bytes 12582916
  14.7 102.3 %copy-start.5 = (bf16[1024,1024]{1,0:T(8,128)(2,1)S(1)}, bf16[1024,1024]{1,0:T(8,128)(2,1)}, u32[]{:S(2)}) copy-start(bf16[1024,1024]{1,0:T(8,128)(2,1)} %param.11) | copy-start | bytes 6291460
  14.7 102.3 %copy-start.6 = (bf16[1024,512]{1,0:T(8,128)(2,1)S(1)}, bf16[1024,512]{1,0:T(8,128)(2,1)}, u32[]{:S(2)}) copy-start(bf16[1024,512]{1,0:T(8,128)(2,1)} %param.12) | copy-start | bytes 3145732
  175.4 15.1 %collective-permute-start.1 = (bf16[256,1024]{1,0:T(8,128)(2,1)}, bf16[256,1024]{1,0:T(8,128)(2,1)}, u32[]{:S(2)}, u32[]{:S(2)}) collective-permute-start(bf16[256,1024]{1,0:T(8,128)(2,1)} %get-tuple-element.21), channel_id=1, source_target_pairs={{0,4},{1,12},{2,20},{3,28},{4,0},{5,8},{6,16},{7,24},{8,5},{9,13},... | collective-permute-start | bytes 1572872 | tf_op jit(solution)/shard_map/ppermute | solution.py:294
  176.9 13.7 %collective-permute-start = (bf16[256,1024]{1,0:T(8,128)(2,1)}, bf16[256,1024]{1,0:T(8,128)(2,1)}, u32[]{:S(2)}, u32[]{:S(2)}) collective-permute-start(bf16[256,1024]{1,0:T(8,128)(2,1)} %get-tuple-element.22), channel_id=1, source_target_pairs={{0,0},{1,8},{2,16},{3,24},{4,4},{5,12},{6,20},{7,28},{8,1},{9,9},{... | collective-permute-start | bytes 1572872 | tf_op jit(solution)/shard_map/ppermute | solution.py:294
  187.3 62.1 %copy-start.1 = (bf16[256,2048]{1,0:T(8,128)(2,1)S(1)}, bf16[256,2048]{1,0:T(8,128)(2,1)}, u32[]{:S(2)}) copy-start(bf16[256,2048]{1,0:T(8,128)(2,1)} %param.13) | copy-start | bytes 3145732
Sparse Core Ops, SparseCore 0:
  128.3 44.8 reduce-scatter.1
where the time goes:
time: 261 us; the launch traced here: 260 us
  Pallas kernels  150 us (57%)
  waiting for transfers between devices  36.6 us (14%)
  matrix products  21.4 us (8%)
  other arithmetic  21.3 us (8%)
  between operations  18.7 us (7%)
  starting transfers between devices  6.88 us (3%)
  local copies, waits for them, and re-layouts  5.84 us (2%)
    pallas_call x1, Pallas kernels, gather(): pl.pallas_call(functools.partial(gather_kernel, n_row, n_col), out_shape=...  102 us
    pallas_call x1, Pallas kernels, sums(): pl.pallas_call(functools.partial(sums_kernel, n_row, n_col), out_shape=(j...  41.3 us
    reduce_scatter x1, waiting for transfers between devices, local(): lax.psum_scatter(partial_value.astype(jnp.bfloat16), 'col', scatter_dimen...  34.7 us
    dot_general x1, matrix products, local(): lax.dot_general(all_cotangents, weights, contract_cols, preferred_element...  11.1 us
    dot_general x1, matrix products, local(): lax.dot_general(columns, all_cotangents, (((0,), (0,)), ((), ())), prefer...  10.3 us
    ppermute x2, starting transfers between devices, local(): arrived.append(lax.ppermute(piece, ('row', 'col'), pairs))  6.84 us
    pallas_call x1, Pallas kernels, total(): pl.pallas_call(functools.partial(total_kernel, n_col), out_shape=jax.Shap...  5.97 us
  transfers between devices with their start and end apart: 3, of which 2 were waited for; matrix products, arithmetic and copies ran while one was open for 6% of the time, Pallas kernels for 0%

commit v1 on v0

v1 whole, which is shorter than its diff:
```python
import functools
import math

import jax
import jax.numpy as jnp
from jax import lax
from jax.experimental import pallas as pl
from jax.experimental.pallas import tpu as pltpu
from jax.sharding import PartitionSpec as P

epsilon = 1e-05
MESH = pl.DeviceIdType.MESH
F32 = jnp.float32
BF16 = jnp.bfloat16
SWAPS = 4


def tile(size, limit):
    return limit if size % limit == 0 else size


def step_kernel(
    n_row, n_col,
    x_hbm, gain, dq_hbm, dk_hbm, wq_hbm, wk_hbm, resid_hbm,
    dinput_hbm, gwq_hbm, gwk_hbm, gains_out, total_out,
    cotq, cotk, xin, normed, ncols, wq, wk, resid, pfull, precv, csend, xrecv, fg,
    gq, gk, dout, inv, sq, dots, dots_in, gains, gains_in, tot, tot_in,
    load_sem, cot_send, cot_recv, swap_send, swap_recv, xs_send, xs_recv,
    cs_send, cs_recv, pe_send, pe_recv, xr_send, xr_recv, fs_send, fs_recv,
    out_sem, dot_send, dot_recv, gain_send, gain_recv, tot_send, tot_recv,
):
    row, col = lax.axis_index("row"), lax.axis_index("col")
    tokens, width = xin.shape
    half = tokens // 2
    part = tokens // n_col
    feats = width // n_row
    slice_width = width // n_col
    fold = n_row // n_col
    n_o, n_x = n_row // 2, n_col // 2
    o, y = row // 2, row % 2
    x, core = col // 2, col % 2
    mate = row + 1 - 2 * y
    home_col = row // fold
    home_x = home_col // 2
    at_home = x == home_x

    def remote(src, dst, send, recv, to_row, to_col):
        return pltpu.make_async_remote_copy(
            src_ref=src, dst_ref=dst, send_sem=send, recv_sem=recv,
            device_id=(to_row, to_col), device_id_type=MESH,
        )

    barrier = pltpu.get_barrier_semaphore()

    def greet_plane(k, carry):
        r = (row + k // 2) % n_row
        c = 2 * x + (core + k % 2) % 2
        pl.semaphore_signal(barrier, inc=1, device_id=(r, c), device_id_type=MESH)
        return carry

    lax.fori_loop(1, 2 * n_row, greet_plane, 0)

    def greet_cols(k, carry):
        c = (2 * x + k) % n_col
        pl.semaphore_signal(barrier, inc=1, device_id=(row, c), device_id_type=MESH)
        return carry

    lax.fori_loop(2, n_col, greet_cols, 0)
    x_copy = pltpu.make_async_copy(x_hbm, xin, load_sem.at[0])
    x_copy.start()
    pl.semaphore_wait(barrier, 2 * n_row - 1 + n_col - 2)

    def block(i):
        return pl.ds(pl.multiple_of(i * tokens, tokens), tokens)

    def nth(j):
        m = jnp.where(o < n_o - 1 - o, o, n_o - 1 - o)
        d = jnp.where(j <= 2 * m, (j + 1) // 2, j - m)
        up = jnp.where(j <= 2 * m, j % 2 == 0, o < n_o - 1 - o)
        return jnp.where(up, o + d, o - d)

    pieces = ((dq_hbm, cotq), (dk_hbm, cotk))

    def cot_copy(j, way, p, source, to_row, own):
        held = pieces[p][1].at[block(source)]
        return remote(
            pieces[p][0] if own else held, held,
            cot_send.at[j, way, p], cot_recv.at[source, p], to_row, col,
        )

    for p in range(2):
        cot_copy(0, 2, p, row, mate, True).start()

        @pl.when(o + 1 < n_o)
        def _():
            cot_copy(0, 0, p, row, row + 2, True).start()

        @pl.when(o > 0)
        def _():
            cot_copy(0, 1, p, row, row - 2, True).start()

    keep = [
        pltpu.make_async_copy(dq_hbm, cotq.at[block(row)], load_sem.at[1]),
        pltpu.make_async_copy(dk_hbm, cotk.at[block(row)], load_sem.at[2]),
        pltpu.make_async_copy(wq_hbm, wq, load_sem.at[3]),
        pltpu.make_async_copy(wk_hbm, wk, load_sem.at[4]),
    ]
    late = pltpu.make_async_copy(resid_hbm, resid, load_sem.at[5])
    x_copy.wait()
    for copy in keep:
        copy.start()
    late.start()

    rows_step = 16

    def norm_rows(i, carry):
        rows = pl.ds(pl.multiple_of(i * rows_step, rows_step), rows_step)
        values = xin[rows, :].astype(F32)
        mean = jnp.sum(values * values, axis=1, keepdims=True) / width
        scale = lax.rsqrt(mean + epsilon)
        inv[rows, :] = jnp.broadcast_to(scale, (rows_step, 128))
        normed[rows, :] = (values * scale * gain[...]).astype(BF16)
        return carry

    lax.fori_loop(0, tokens // rows_step, norm_rows, 0)
    own_cols = pl.ds(pl.multiple_of(row * feats, feats), feats)
    ncols[block(row), :] = normed[:, own_cols]
    for copy in keep:
        copy.wait()

    def quarter(source, c):
        start = pl.multiple_of(source * tokens + c * part, part)
        return ncols.at[pl.ds(start, part)]

    def swap_copy(k):
        target = (row + k) % n_row
        src = normed.at[
            pl.ds(pl.multiple_of(col * part, part), part),
            pl.ds(pl.multiple_of(target * feats, feats), feats),
        ]
        return remote(
            src, quarter(row, col), swap_send.at[k], swap_recv.at[row], target, col
        )

    def swap_arrival(source):
        return remote(
            quarter(source, col), quarter(source, col),
            swap_send.at[0], swap_recv.at[source], row, 2 * x + 1 - core,
        )

    def x_share(source, i):
        to_x = (x + i) % n_x
        return remote(
            quarter(source, col), quarter(source, col),
            xs_send.at[source, i], xs_recv.at[source, x], row, 2 * to_x + core,
        )

    def x_arrival(source, i):
        c = 2 * ((x + n_x - i) % n_x) + core
        return remote(
            quarter(source, c), quarter(source, c),
            xs_send.at[source, i], xs_recv.at[source, (x + n_x - i) % n_x],
            row, 2 * x + 1 - core,
        )

    def core_share(source, from_x, c):
        return remote(
            quarter(source, c), quarter(source, c),
            cs_send.at[source, from_x], cs_recv.at[source, from_x],
            row, 2 * x + 1 - core,
        )

    def swap_step(j, base, action):
        def one(i, carry):
            k = SWAPS * (j - base) + i + 1

            @pl.when((k >= 1) & (k < n_row))
            def _():
                action(k)

            return carry

        lax.fori_loop(0, SWAPS, one, 0)

    def share_first(k):
        source = (row + n_row - k) % n_row
        swap_arrival(source).wait_recv()
        for i in range(1, n_x):
            x_share(source, i).start()
        core_share(source, x, col).start()

    def share_second(k):
        source = (row + n_row - k) % n_row
        for i in range(1, n_x):
            x_arrival(source, i).wait_recv()
            from_x = (x + n_x - i) % n_x
            core_share(source, from_x, 2 * from_x + core).start()

    contract = (((1,), (1,)), ((), ()))
    f_tile = tile(feats, 256)
    own_half = pl.multiple_of(core * half, half)
    other_half = pl.multiple_of((1 - core) * half, half)

    def half_rows(source, start):
        return pl.ds(pl.multiple_of(source * tokens + start, half), half)

    def slot(source):
        return pl.ds(pl.multiple_of(source * half, half), half)

    def pair_copy(source):
        return remote(
            pfull.at[half_rows(source, other_half)], precv.at[slot(source)],
            pe_send.at[source], pe_recv.at[source], row, 2 * x + 1 - core,
        )

    def cross_copy(source):
        return remote(
            csend.at[slot(source)], xrecv.at[x, slot(source)],
            xr_send.at[source], xr_recv.at[x, source], row, 2 * home_x + core,
        )

    def home_copy(source):
        return remote(
            csend.at[slot(source)], fg.at[row % fold, pl.ds(own_half, half)],
            fs_send.at[source], fs_recv.at[row % fold, core], source, home_col,
        )

    def stage_one(source):
        def one(i, carry):
            fs = pl.ds(pl.multiple_of(i * f_tile, f_tile), f_tile)
            value = lax.dot_general(
                cotq[block(source), :], wq[fs, :], contract, preferred_element_type=F32
            ) + lax.dot_general(
                cotk[block(source), :], wk[fs, :], contract, preferred_element_type=F32
            )
            pfull[block(source), fs] = value.astype(BF16)
            return carry

        lax.fori_loop(0, feats // f_tile, one, 0)
        pair_copy(source).start()

    add_rows = tile(half, 32)

    def stage_two(source):
        pair_copy(source).wait_recv()

        @pl.when(jnp.logical_not(at_home))
        def _():
            def one(i, carry):
                at = i * add_rows
                mine = pl.ds(pl.multiple_of(source * tokens + own_half + at, add_rows), add_rows)
                rows = pl.ds(pl.multiple_of(source * half + at, add_rows), add_rows)
                value = pfull[mine, :].astype(F32) + precv[rows, :].astype(F32)
                csend[rows, :] = value.astype(BF16)
                return carry

            lax.fori_loop(0, half // add_rows, one, 0)
            cross_copy(source).start()

    def stage_three(source):
        @pl.when(at_home)
        def _():
            for i in range(1, n_x):
                from_x = (x + i) % n_x
                remote(
                    csend.at[slot(source)], xrecv.at[from_x, slot(source)],
                    xr_send.at[source], xr_recv.at[from_x, source],
                    row, 2 * x + 1 - core,
                ).wait_recv()

            def one(i, carry):
                at = i * add_rows
                mine = pl.ds(pl.multiple_of(source * tokens + own_half + at, add_rows), add_rows)
                rows = pl.ds(pl.multiple_of(source * half + at, add_rows), add_rows)
                value = pfull[mine, :].astype(F32) + precv[rows, :].astype(F32)
                for k in range(1, n_x):
                    value = value + xrecv[(x + k) % n_x, rows, :].astype(F32)
                csend[rows, :] = value.astype(BF16)
                return carry

            lax.fori_loop(0, half // add_rows, one, 0)
            here = (source == row) & (home_col == col)

            @pl.when(jnp.logical_not(here))
            def _():
                home_copy(source).start()

            @pl.when(here)
            def _():
                fg[row % fold, pl.ds(own_half, half), :] = csend[slot(source), :]

    down = (((0,), (0,)), ((), ()))
    weight_scale = 1.0 / math.sqrt(tokens)
    groups = []
    for held, kept, out in ((cotq, gq, gwq_hbm), (cotk, gk, gwk_hbm)):
        groups.append((held, kept, out, tile(held.shape[1], 512)))

    def out_copy(g, fs, i):
        _, kept, out, _ = groups[g]
        return pltpu.make_async_copy(kept.at[fs], out.at[fs], out_sem.at[g, i])

    def weight_tile(i, carry):
        fs = pl.ds(pl.multiple_of(i * f_tile, f_tile), f_tile)
        for g, (held, kept, _, k_tile) in enumerate(groups):
            for k in range(held.shape[1] // k_tile):
                ks = pl.ds(k * k_tile, k_tile)
                value = lax.dot_general(
                    ncols[:, fs], held[:, ks], down, preferred_element_type=F32
                )
                value = (value * weight_scale).astype(BF16)
                kept[fs, ks] = value
                value = value.astype(F32)
                value = jnp.sum(value * value, axis=0, keepdims=True)
                for part_at in range(k_tile // 128):
                    sq[...] += value[:, part_at * 128 : (part_at + 1) * 128]
            out_copy(g, fs, i).start()
        return carry

    f_tiles = feats // f_tile
    early_tiles = f_tiles // 2
    sq[...] = jnp.zeros_like(sq)

    def main_step(j, carry):
        @pl.when((j >= 1) & (j < n_o))
        def _():
            line = nth(j)
            source = 2 * line + y
            rising = line < o
            onward = jnp.where(rising, o + 1 < n_o, o > 0)
            to_row = jnp.where(rising, row + 2, row - 2)
            for p in range(2):
                cot_copy(j, 0, p, source, mate, False).wait_recv()

                @pl.when(onward)
                def _():
                    cot_copy(j, 0, p, source, to_row, False).start()

                cot_copy(j, 2, p, source, mate, False).start()

        swap_step(j, 0, lambda k: swap_copy(k).start())
        swap_step(j, 2, share_first)
        swap_step(j, 3, share_second)

        def source_of(b):
            return 2 * nth(j - b) + jnp.where(b == 0, y, 1 - y)

        def each(action):
            def one(b, carry):
                @pl.when(jnp.where(b == 0, j < n_o, j >= 1))
                def _():
                    action(source_of(b), b)

                return carry

            lax.fori_loop(0, 2, one, 0)

        def first(source, b):
            @pl.when(b == 1)
            def _():
                for p in range(2):
                    cot_copy(0, 0, p, source, mate, False).wait_recv()

            stage_one(source)

        each(first)
        each(lambda source, b: stage_two(source))

        @pl.when(j == n_o)
        def _():
            def wait_one(k, carry):
                source = (row + k) % n_row
                for from_x in range(n_x):
                    core_share(source, from_x, 2 * from_x + 1 - core).wait_recv()
                return carry

            lax.fori_loop(1, n_row, wait_one, 0)
            lax.fori_loop(0, early_tiles, weight_tile, 0)

        each(lambda source, b: stage_three(source))
        return carry

    lax.fori_loop(0, n_o + 1, main_step, 0)
    lax.fori_loop(early_tiles, f_tiles, weight_tile, 0)

    for j in range(fold):
        for c in range(2):
            @pl.when(jnp.logical_not((col * fold + j == row) & (c == core)))
            def _():
                arrived = fg.at[j, pl.ds(c * half, half)]
                remote(
                    arrived, arrived, fs_send.at[0], fs_recv.at[j, c], row, 2 * x + 1 - core
                ).wait_recv()

    late.wait()
    col_start = col * slice_width
    c_tile = tile(feats, 256)
    model_width = width
    tiles = feats // c_tile

    def lanes(value):
        total = value[:, 0:128]
        for k in range(1, c_tile // 128):
            total = total + value[:, k * 128 : (k + 1) * 128]
        return total

    def wide(value):
        return jnp.concatenate([value] * (c_tile // 128), axis=1)

    acc = jnp.zeros((tokens, 128), F32)
    for j in range(fold):
        for t in range(tiles):
            at = j * feats + t * c_tile
            here = pl.ds(pl.multiple_of(col_start + at, 128), c_tile)
            product = fg[j, :, t * c_tile : (t + 1) * c_tile].astype(F32) * xin[:, here].astype(F32)
            acc = acc + lanes(product * gain[:, here])
            gains[:, at : at + c_tile] = jnp.sum(product * wide(inv[...]), axis=0, keepdims=True)
    summed = jnp.broadcast_to(jnp.sum(acc, axis=1, keepdims=True), (tokens, 128))
    dots[...] = jnp.transpose(summed)[0:8, :]
    gains[:, slice_width:] = sq[...]

    dot_copies, gain_copies = [], []
    for k in range(1, n_col):
        dot_copies.append(
            remote(dots, dots_in.at[col], dot_send.at[k], dot_recv.at[k], row, (col + k) % n_col)
        )
    for k in range(1, n_row):
        gain_copies.append(
            remote(gains, gains_in.at[row], gain_send.at[k], gain_recv.at[k], (row + k) % n_row, col)
        )
    for copy in dot_copies + gain_copies:
        copy.start()
    dots_in[col] = dots[...]
    gains_in[row] = gains[...]
    for copy in gain_copies:
        copy.wait()
    all_gains = jnp.sum(gains_in[...], axis=0)
    grad_gain = all_gains[:, :slice_width] * (1.0 / math.sqrt(tokens * n_row))
    gains_out[...] = grad_gain
    squares = jnp.sum(grad_gain * grad_gain) + jnp.sum(all_gains[:, slice_width:])
    tot[...] = jnp.full(tot.shape, squares, F32)
    tot_copies = [
        remote(tot, tot_in.at[col], tot_send.at[k], tot_recv.at[k], row, (col + k) % n_col)
        for k in range(1, n_col)
    ]
    for copy in tot_copies:
        copy.start()
    tot_in[col] = tot[...]
    for copy in dot_copies:
        copy.wait()
    token_row = jnp.sum(dots_in[...], axis=0)[0:1, :]
    token_dot = jnp.transpose(jnp.broadcast_to(token_row, (128, tokens)))
    inv_rms = inv[...]
    inv_wide = wide(inv_rms)
    factor = wide(inv_rms * inv_rms * inv_rms * token_dot / model_width)
    d_copies = []
    for j in range(fold):
        for t in range(tiles):
            at = j * feats + t * c_tile
            here = pl.ds(pl.multiple_of(col_start + at, 128), c_tile)
            grad = fg[j, :, t * c_tile : (t + 1) * c_tile].astype(F32)
            value = (
                resid[:, at : at + c_tile].astype(F32)
                + inv_wide * gain[:, here] * grad
                - xin[:, here].astype(F32) * factor
            )
            dout[:, at : at + c_tile] = value.astype(BF16)
        span = pl.ds(j * feats, feats)
        copy = pltpu.make_async_copy(dout.at[:, span], dinput_hbm.at[:, span], load_sem.at[6 + j])
        copy.start()
        d_copies.append(copy)
    for copy in tot_copies:
        copy.wait()
    total_out[...] = jnp.sum(tot_in[...], axis=0) / model_width

    for copy in d_copies:
        copy.wait()
    for g in range(2):
        for i in range(f_tiles):
            out_copy(g, pl.ds(i * f_tile, f_tile), i).wait()
    for p in range(2):
        cot_copy(0, 2, p, row, mate, True).wait_send()

        @pl.when(o + 1 < n_o)
        def _():
            cot_copy(0, 0, p, row, row + 2, True).wait_send()

        @pl.when(o > 0)
        def _():
            cot_copy(0, 1, p, row, row - 2, True).wait_send()

    def drain_line(j, carry):
        line = nth(j)
        onward = jnp.where(line < o, o + 1 < n_o, o > 0)
        for p in range(2):
            cot_copy(j, 2, p, 2 * line + y, mate, False).wait_send()

            @pl.when(onward)
            def _():
                cot_copy(j, 0, p, 2 * line + y, mate, False).wait_send()

        return carry

    lax.fori_loop(1, n_o, drain_line, 0)

    def drain_row(k, carry):
        source = (row + k) % n_row
        pair_copy(source).wait_send()

        @pl.when(jnp.logical_not(at_home))
        def _():
            cross_copy(source).wait_send()

        @pl.when(at_home & jnp.logical_not((source == row) & (home_col == col)))
        def _():
            home_copy(source).wait_send()

        @pl.when(k >= 1)
        def _():
            swap_copy(k).wait_send()
            for i in range(1, n_x):
                x_share(source, i).wait_send()
            for from_x in range(n_x):
                core_share(source, from_x, col).wait_send()

        return carry

    lax.fori_loop(0, n_row, drain_row, 0)


def local(layer_input, gain, d_query, d_keyval, w_query, w_keyval, d_resid):
    n_row, n_col = lax.axis_size("row"), lax.axis_size("col")
    n_x, n_o, fold = n_col // 2, n_row // 2, n_row // n_col
    tokens, width = layer_input.shape
    q_cols, k_cols = d_query.shape[1], d_keyval.shape[1]
    feats, slice_width = width // n_row, width // n_col
    half = tokens // 2
    f_tiles = feats // tile(feats, 256)
    dma = pltpu.SemaphoreType.DMA
    hbm = pl.BlockSpec(memory_space=pl.ANY)
    vmem = pl.BlockSpec(memory_space=pltpu.VMEM)
    shape = jax.ShapeDtypeStruct
    every = n_row * tokens
    d_input, grad_wq, grad_wkv, grad_gain, total = pl.pallas_call(
        functools.partial(step_kernel, n_row, n_col),
        out_shape=(
            shape((tokens, slice_width), BF16),
            shape((feats, q_cols), BF16),
            shape((feats, k_cols), BF16),
            shape((1, slice_width), F32),
            shape((1, 128), F32),
        ),
        in_specs=[hbm, vmem, hbm, hbm, hbm, hbm, hbm],
        out_specs=[hbm, hbm, hbm, vmem, vmem],
        scratch_shapes=[
            pltpu.VMEM((every, q_cols), BF16),
            pltpu.VMEM((every, k_cols), BF16),
            pltpu.VMEM((tokens, width), BF16),
            pltpu.VMEM((tokens, width), BF16),
            pltpu.VMEM((every, feats), BF16),
            pltpu.VMEM((feats, q_cols), BF16),
            pltpu.VMEM((feats, k_cols), BF16),
            pltpu.VMEM((tokens, slice_width), BF16),
            pltpu.VMEM((every, feats), BF16),
            pltpu.VMEM((n_row * half, feats), BF16),
            pltpu.VMEM((n_row * half, feats), BF16),
            pltpu.VMEM((n_x, n_row * half, feats), BF16),
            pltpu.VMEM((fold, tokens, feats), BF16),
            pltpu.VMEM((feats, q_cols), BF16),
            pltpu.VMEM((feats, k_cols), BF16),
            pltpu.VMEM((tokens, slice_width), BF16),
            pltpu.VMEM((tokens, 128), F32),
            pltpu.VMEM((1, 128), F32),
            pltpu.VMEM((8, tokens), F32),
            pltpu.VMEM((n_col, 8, tokens), F32),
            pltpu.VMEM((1, slice_width + 128), F32),
            pltpu.VMEM((n_row, 1, slice_width + 128), F32),
            pltpu.VMEM((1, 128), F32),
            pltpu.VMEM((n_col, 1, 128), F32),
            dma((6 + fold,)),
            dma((n_o, 3, 2)),
            dma((n_row, 2)),
            dma((n_row,)),
            dma((n_row,)),
            dma((n_row, n_x)),
            dma((n_row, n_x)),
            dma((n_row, n_x)),
            dma((n_row, n_x)),
            dma((n_row,)),
            dma((n_row,)),
            dma((n_row,)),
            dma((n_x, n_row)),
            dma((n_row,)),
            dma((fold, 2)),
            dma((2, f_tiles)),
            dma((n_col,)),
            dma((n_col,)),
            dma((n_row,)),
            dma((n_row,)),
            dma((n_col,)),
            dma((n_col,)),
        ],
        compiler_params=pltpu.CompilerParams(
            collective_id=0, has_side_effects=True, vmem_limit_bytes=63 * 1024 * 1024
        ),
        name="step",
    )(layer_input, gain.reshape(1, width), d_query, d_keyval, w_query, w_keyval, d_resid)
    return (d_input, grad_wq, grad_wkv, grad_gain.reshape(slice_width), total[0, 0])


def solution(mesh):
    placed = (
        P("row", None),
        P(),
        P("row", "col"),
        P("row", "col"),
        P("row", "col"),
        P("row", "col"),
        P("row", "col"),
    )
    return jax.shard_map(
        local,
        mesh=mesh,
        in_specs=placed,
        out_specs=(P("row", "col"), P("row", "col"), P("row", "col"), P("col"), P()),
        check_vma=False,
    )
```

time: 261 us -> 143 us (0.55)
  waiting for transfers between devices: 36.6 us -> 0 us
  matrix products: 21.4 us -> 0 us
  other arithmetic: 21.3 us -> 0 us
  between operations: 18.7 us -> 1.82 us
  Pallas kernels: 150 us -> 135 us
  starting transfers between devices: 6.88 us -> 0 us
    reduce_scatter x1 -> x0, waiting for transfers between devices: 34.7 us -> none  [local(): lax.psum_scatter(partial_value.astype(jnp.bfloat16), 'col', scatter_dimen...]
    dot_general x2 -> x0, matrix products: 21.4 us -> none  [the longest x1 11.1 us: local(): lax.dot_general(all_cotangents, weights, contract_cols, preferred_element...]
    pallas_call x3 -> x1, Pallas kernels: 150 us -> 135 us  [local(): pl.pallas_call(functools.partial(step_kernel, n_row, n_col), out_shape=(s...]
    reduce_sum x5 -> x0, other arithmetic: 12.6 us -> none  [the longest x2 4.98 us: local(): tile_square = jnp.sum(query_f * query_f) + jnp.sum(keyval_f * keyval_f)]
    ppermute x2 -> x0, starting transfers between devices: 6.84 us -> none  [local(): arrived.append(lax.ppermute(piece, ('row', 'col'), pairs))]
    convert_element_type x2 -> x0, other arithmetic: 6.24 us -> none  [the longest x1 3.26 us: local(): normed = (inputs * inv_rms * gain).astype(jnp.bfloat16)]
    unnamed x14 -> x12, local copies, waits for them, and re-layouts: 0.03 us -> 5.99 us
  transfers between devices with their start and end apart: 3 -> 0, of which waited for: 2 -> 0; matrix products, arithmetic and copies ran while one was open for 6% -> 0% of each run, Pallas kernels for 0% -> 0%
where the time goes in v1:
time: 143 us; the launch traced here: 142 us
  Pallas kernels  135 us (94%)
  local copies, waits for them, and re-layouts  5.99 us (4%)
  between operations  1.82 us (1%)
    pallas_call x1, Pallas kernels, local(): pl.pallas_call(functools.partial(step_kernel, n_row, n_col), out_shape=(s...  135 us
    unnamed x12, local copies, waits for them, and re-layouts  5.99 us

profile of v1, /device:TPU:0, one launch (start us, length us, event | category | flops | bytes accessed | tf_op | source)
XLA Modules:
  0.0 142.4 jit_solution(8557353608305106781)
XLA Ops:
  0.6 134.6 %step.1 = (bf16[256,2048]{1,0:T(8,128)(2,1)}, bf16[1024,1024]{1,0:T(8,128)(2,1)}, bf16[1024,512]{1,0:T(8,128)(2,1)}, f32[1,2048]{1,0:T(1,128)}, f32[1,128]{1,0:T(1,128)}) custom-call(bf16[256,8192]{1,0:T(8,128)(2,1)} %x_hbm.1, f32[1,8192]{1,0:T(1,128)} %bitcast.4, bf16[256,1024]{1,0:T(8,128)(2,1)} %dq_hbm.1, bf16[256,512]{1,0:T(8,128)(2,1)} %dk_hbm.1, ...), custom_call_target="tpu_custom_call" | custom-call | tf_op jit(solution)/shard_map/step/pallas_call | solution.py:543
  135.2 0.0 copy-start
  135.2 2.5 %copy.17 = bf16[256,2048]{1,0:T(8,128)(2,1)} copy(bf16[256,2048]{1,0:T(8,128)(2,1)} %get-tuple-element.20) | data formatting | bytes 2097152
  137.7 0.0 copy-done
  137.7 0.0 copy-start.1
  137.7 1.3 copy.18
  139.0 0.6 copy-done.1
  139.7 0.0 copy-start.2
  139.7 0.0 copy-start.3
  139.7 1.0 copy.19
  140.6 0.0 copy-done.2
  140.6 0.6 copy.20
  141.2 0.0 copy-done.3
Async XLA Ops:
  135.2 2.5 %copy-start = (bf16[1024,1024]{1,0:T(8,128)(2,1)S(1)}, bf16[1024,1024]{1,0:T(8,128)(2,1)}, u32[]{:S(2)}) copy-start(bf16[1024,1024]{1,0:T(8,128)(2,1)} %get-tuple-element.21) | copy-start | bytes 6291460
  137.7 2.0 %copy-start.1 = (bf16[1024,512]{1,0:T(8,128)(2,1)S(1)}, bf16[1024,512]{1,0:T(8,128)(2,1)}, u32[]{:S(2)}) copy-start(bf16[1024,512]{1,0:T(8,128)(2,1)} %get-tuple-element.22) | copy-start | bytes 3145732
  139.7 1.0 copy-start.2
  139.7 1.6 %copy-start.3 = (f32[1,128]{1,0:T(1,128)S(1)}, f32[1,128]{1,0:T(1,128)}, u32[]{:S(2)}) copy-start(f32[1,128]{1,0:T(1,128)} %get-tuple-element.14) | copy-start | bytes 1540

commit v2 on v1

v2 whole, which is shorter than its diff:
```python
import functools
import math

import jax
import jax.numpy as jnp
from jax import lax
from jax.experimental import pallas as pl
from jax.experimental.pallas import tpu as pltpu
from jax.sharding import PartitionSpec as P

epsilon = 1e-05
MESH = pl.DeviceIdType.MESH
F32 = jnp.float32
BF16 = jnp.bfloat16
VMEM_LIMIT = 48 * 1024 * 1024


def tile(size, limit):
    return limit if size % limit == 0 else size


def step_kernel(
    n_row, n_col,
    x_hbm, gain_hbm, dq_hbm, dk_hbm, wq_hbm, wk_hbm, resid_hbm,
    dout, gq, gk, gains_out, total_out,
    cotq, cotk, xin, normed, ncols, wq, wk, resid, pfull, precv, csend, xrecv, fg,
    gain, acc_q, acc_k, inv, sq, dots, dots_in, gains, gains_in, tot, tot_in,
    load_sem, cot_send, cot_recv, swap_send, swap_recv, xs_send,
    cs_send, cs_recv, pe_send, pe_recv, xr_send, xr_recv, fs_send, fs_recv,
    dot_send, dot_recv, gain_send, gain_recv, tot_send, tot_recv,
):
    row, col = lax.axis_index("row"), lax.axis_index("col")
    tokens, width = xin.shape
    half = tokens // 2
    feats = width // n_row
    slice_width = width // n_col
    fold = n_row // n_col
    n_o, n_x = n_row // 2, n_col // 2
    o, y = row // 2, row % 2
    x, core = col // 2, col % 2
    mate = row + 1 - 2 * y
    home_col = row // fold
    home_x = home_col // 2
    at_home = x == home_x
    swap_x = (home_x + n_x // 2) % n_x
    halves = fg.shape[1]

    def remote(src, dst, send, recv, to_row, to_col):
        return pltpu.make_async_remote_copy(
            src_ref=src, dst_ref=dst, send_sem=send, recv_sem=recv,
            device_id=(to_row, to_col), device_id_type=MESH,
        )

    barrier = pltpu.get_barrier_semaphore()

    def greet_plane(k, carry):
        r = (row + k // 2) % n_row
        c = 2 * x + (core + k % 2) % 2
        pl.semaphore_signal(barrier, inc=1, device_id=(r, c), device_id_type=MESH)
        return carry

    lax.fori_loop(1, 2 * n_row, greet_plane, 0)

    def greet_cols(k, carry):
        c = (2 * x + k) % n_col
        pl.semaphore_signal(barrier, inc=1, device_id=(row, c), device_id_type=MESH)
        return carry

    lax.fori_loop(2, n_col, greet_cols, 0)
    x_copy = pltpu.make_async_copy(x_hbm, xin, load_sem.at[0])
    x_copy.start()
    gain_copy = pltpu.make_async_copy(gain_hbm, gain, load_sem.at[6])
    gain_copy.start()
    with jax.named_scope("greet"):
        pl.semaphore_wait(barrier, 2 * n_row - 1 + n_col - 2)

    def place(i):
        return (i % 2) * n_o + i // 2

    def block(i):
        return pl.ds(pl.multiple_of(place(i) * tokens, tokens), tokens)

    def nth(j):
        m = jnp.where(o < n_o - 1 - o, o, n_o - 1 - o)
        d = jnp.where(j <= 2 * m, (j + 1) // 2, j - m)
        up = jnp.where(j <= 2 * m, j % 2 == 0, o < n_o - 1 - o)
        return jnp.where(up, o + d, o - d)

    pieces = ((dq_hbm, cotq), (dk_hbm, cotk))

    def cot_copy(way, p, source, to_row, own):
        held = pieces[p][1].at[block(source)]
        return remote(
            pieces[p][0] if own else held, held,
            cot_send.at[source // 2, way, p], cot_recv.at[source, p], to_row, col,
        )

    for p in range(2):
        cot_copy(2, p, row, mate, True).start()

        @pl.when(o + 1 < n_o)
        def _():
            cot_copy(0, p, row, row + 2, True).start()

        @pl.when(o > 0)
        def _():
            cot_copy(1, p, row, row - 2, True).start()

    keep = [
        pltpu.make_async_copy(dq_hbm, cotq.at[block(row)], load_sem.at[1]),
        pltpu.make_async_copy(dk_hbm, cotk.at[block(row)], load_sem.at[2]),
        pltpu.make_async_copy(wq_hbm, wq, load_sem.at[3]),
        pltpu.make_async_copy(wk_hbm, wk, load_sem.at[4]),
    ]
    late = pltpu.make_async_copy(resid_hbm, resid, load_sem.at[5])
    x_copy.wait()
    gain_copy.wait()
    for copy in keep:
        copy.start()
    late.start()

    rows_step = 16

    def norm_rows(i, carry):
        rows = pl.ds(pl.multiple_of(i * rows_step, rows_step), rows_step)
        values = xin[rows, :].astype(F32)
        mean = jnp.sum(values * values, axis=1, keepdims=True) / width
        scale = lax.rsqrt(mean + epsilon)
        inv[rows, :] = jnp.broadcast_to(scale, (rows_step, 128))
        normed[rows, :] = (values * scale * gain[...]).astype(BF16)
        return carry

    with jax.named_scope("norm"):
        lax.fori_loop(0, tokens // rows_step, norm_rows, 0)
    own_cols = pl.ds(pl.multiple_of(row * feats, feats), feats)
    ncols[block(row), :] = normed[:, own_cols]
    for copy in keep:
        copy.wait()

    def rows_of(source, c):
        return ncols.at[pl.ds(pl.multiple_of(place(source) * tokens + c * half, half), half)]

    def swap_plane(source):
        return (source // fold // 2 + n_x // 2) % n_x

    def swap_copy(target):
        src = normed.at[
            pl.ds(pl.multiple_of(core * half, half), half),
            pl.ds(pl.multiple_of(target * feats, feats), feats),
        ]
        return remote(
            src, rows_of(row, core), swap_send.at[target], swap_recv.at[row], target, col
        )

    def x_share(source, i):
        mine = rows_of(source, core)
        to_x = (x + i) % n_x
        return remote(
            mine, mine, xs_send.at[source, i], swap_recv.at[source], row, 2 * to_x + core
        )

    def core_share(source):
        mine = rows_of(source, core)
        return remote(
            mine, mine, cs_send.at[source], cs_recv.at[source], row, 2 * x + 1 - core
        )

    def swap_start(target):
        @pl.when(x == swap_x)
        def _():
            swap_copy(target).start()

    def line_peer(k):
        shift = jnp.where(o < n_o // 2, k, n_o - k)
        return 2 * ((o + shift) % n_o) + y

    def mate_peer(k):
        return 2 * ((o + k) % n_o) + 1 - y

    def take(source):
        mine = rows_of(source, core)
        with jax.named_scope("wait_swap"):
            remote(
                mine, mine, cs_send.at[source], swap_recv.at[source], row, 2 * x + 1 - core
            ).wait_recv()
        core_share(source).start()

    def share_first(source):
        @pl.when(x == swap_plane(source))
        def _():
            take(source)
            for i in range(1, n_x):
                x_share(source, i).start()

    def share_second(source):
        @pl.when(x != swap_plane(source))
        def _():
            take(source)

    def first_shares(peer, start):
        def one(k, carry):
            share_first(peer(k))
            return carry

        lax.fori_loop(start, n_o, one, 0)

    def second_shares(peer, start):
        def one(k, carry):
            share_second(peer(k))
            return carry

        def wait(k, carry):
            core_share(peer(k)).wait_recv()
            return carry

        lax.fori_loop(start, n_o, one, 0)
        with jax.named_scope("wait_share"):
            lax.fori_loop(start, n_o, wait, 0)

    contract = (((1,), (1,)), ((), ()))
    f_tile = tile(feats, 256)
    own_half = pl.multiple_of(core * half, half)
    other_half = pl.multiple_of((1 - core) * half, half)

    def half_rows(source, start):
        return pl.ds(pl.multiple_of(place(source) * tokens + start, half), half)

    def slot(source):
        return pl.ds(pl.multiple_of(source * half, half), half)

    def pair_copy(source, h):
        return remote(
            pfull.at[h, half_rows(source, other_half)], precv.at[h, slot(source)],
            pe_send.at[source, h], pe_recv.at[source, h], row, 2 * x + 1 - core,
        )

    def cross_copy(source, h):
        return remote(
            csend.at[h, slot(source)], xrecv.at[x, h, slot(source)],
            xr_send.at[source, h], xr_recv.at[x, source, h], row, 2 * home_x + core,
        )

    def home_copy(source, h):
        return remote(
            csend.at[h, slot(source)], fg.at[row % fold, h, pl.ds(own_half, half)],
            fs_send.at[source, h], fs_recv.at[row % fold, h, core], source, home_col,
        )

    h_width = feats // halves
    h_tiles = h_width // f_tile

    def stage_one(source, h):
        def one(i, carry):
            fs = pl.ds(pl.multiple_of(h * h_width + i * f_tile, f_tile), f_tile)
            value = lax.dot_general(
                cotq[block(source), :], wq[fs, :], contract, preferred_element_type=F32
            ) + lax.dot_general(
                cotk[block(source), :], wk[fs, :], contract, preferred_element_type=F32
            )
            to = pl.ds(pl.multiple_of(i * f_tile, f_tile), f_tile)
            pfull[h, block(source), to] = value.astype(BF16)
            return carry

        with jax.named_scope("multiply"):
            lax.fori_loop(0, h_tiles, one, 0)
        pair_copy(source, h).start()

    add_rows = tile(half, 32)

    def stage_two(source, h):
        with jax.named_scope("wait_pair"):
            pair_copy(source, h).wait_recv()

        @pl.when(jnp.logical_not(at_home))
        def _():
            def one(i, carry):
                at = i * add_rows
                mine = pl.ds(pl.multiple_of(place(source) * tokens + own_half + at, add_rows), add_rows)
                rows = pl.ds(pl.multiple_of(source * half + at, add_rows), add_rows)
                value = pfull[h, mine, :].astype(F32) + precv[h, rows, :].astype(F32)
                csend[h, rows, :] = value.astype(BF16)
                return carry

            lax.fori_loop(0, half // add_rows, one, 0)
            cross_copy(source, h).start()

    def stage_three(source, h):
        @pl.when(at_home)
        def _():
            for i in range(1, n_x):
                from_x = (x + i) % n_x
                with jax.named_scope("wait_cross"):
                    remote(
                        csend.at[h, slot(source)], xrecv.at[from_x, h, slot(source)],
                        xr_send.at[source, h], xr_recv.at[from_x, source, h],
                        row, 2 * x + 1 - core,
                    ).wait_recv()

            def one(i, carry):
                at = i * add_rows
                mine = pl.ds(pl.multiple_of(place(source) * tokens + own_half + at, add_rows), add_rows)
                rows = pl.ds(pl.multiple_of(source * half + at, add_rows), add_rows)
                value = pfull[h, mine, :].astype(F32) + precv[h, rows, :].astype(F32)
                for k in range(1, n_x):
                    value = value + xrecv[(x + k) % n_x, h, rows, :].astype(F32)
                csend[h, rows, :] = value.astype(BF16)
                return carry

            lax.fori_loop(0, half // add_rows, one, 0)
            here = (source == row) & (home_col == col)

            @pl.when(jnp.logical_not(here))
            def _():
                home_copy(source, h).start()

            @pl.when(here)
            def _():
                fg[row % fold, h, pl.ds(own_half, half), :] = csend[h, slot(source), :]

    down = (((0,), (0,)), ((), ()))
    weight_scale = 1.0 / math.sqrt(tokens)
    groups = []
    for held, kept, total in ((cotq, gq, acc_q), (cotk, gk, acc_k)):
        groups.append((held, kept, total, tile(held.shape[1], 512)))
    line_rows = n_o * tokens

    def products(i, line, action):
        fs = pl.ds(pl.multiple_of(i * f_tile, f_tile), f_tile)
        rows = pl.ds(pl.multiple_of(line * line_rows, line_rows), line_rows)
        for held, kept, total, k_tile in groups:
            for k in range(held.shape[1] // k_tile):
                ks = pl.ds(k * k_tile, k_tile)
                value = lax.dot_general(
                    ncols[rows, fs], held[rows, ks], down, preferred_element_type=F32
                )
                action(value, kept, total, fs, ks, k_tile)

    def line_weights(i, carry):
        def keep_sum(value, kept, total, fs, ks, k_tile):
            total[fs, ks] = value

        products(i, y, keep_sum)
        return carry

    def mate_weights(i, carry):
        def finish(value, kept, total, fs, ks, k_tile):
            value = ((value + total[fs, ks]) * weight_scale).astype(BF16)
            kept[fs, ks] = value
            value = value.astype(F32)
            value = jnp.sum(value * value, axis=0, keepdims=True)
            for at in range(0, k_tile, 128):
                sq[...] += value[:, at : at + 128]

        products(i, 1 - y, finish)
        return carry

    f_tiles = feats // f_tile
    sq[...] = jnp.zeros_like(sq)

    def line_source(j):
        return 2 * nth(j) + y

    def mate_source(j):
        return 2 * nth(j) + 1 - y

    def halves_of(source, action):
        def one(h, carry):
            action(source, h)
            return carry

        lax.fori_loop(0, halves, one, 0)

    def mate_arrival(source):
        for p in range(2):
            with jax.named_scope("wait_mate"):
                cot_copy(0, p, source, mate, False).wait_recv()

    at_end = (o == 0) | (o == n_o - 1)

    def swap_if(target, end):
        line = target // 2

        @pl.when(((line == 0) | (line == n_o - 1)) == end)
        def _():
            swap_start(target)

    def swap_all(peer, start, end):
        def one(k, carry):
            swap_if(peer(k), end)
            return carry

        lax.fori_loop(start, n_o, one, 0)

    def sides(j, action):
        def one(side, carry):
            line = jnp.where(side == 0, o - j, o + j)

            @pl.when((line >= 0) & (line < n_o) & ((j > 0) | (side == 0)))
            def _():
                action(line, side)

            return carry

        lax.fori_loop(0, 2, one, 0)

    def arrive(line, side):
        source = 2 * line + y
        onward = jnp.where(side == 0, o + 1 < n_o, o > 0)
        to_row = jnp.where(side == 0, row + 2, row - 2)
        for p in range(2):
            with jax.named_scope("wait_line"):
                cot_copy(0, p, source, mate, False).wait_recv()

            @pl.when(onward)
            def _():
                cot_copy(0, p, source, to_row, False).start()

            cot_copy(2, p, source, mate, False).start()

    def go_home(line, held):
        late_one = ((line == 0) | (line == n_o - 1)) & jnp.logical_not(at_end)

        @pl.when(late_one == held)
        def _():
            halves_of(2 * line + y, stage_three)

    def main_step(j, carry):
        @pl.when(j >= 1)
        def _():
            sides(j, arrive)
            sides(j - 1, lambda line, side: go_home(line, False))

            @pl.when(at_end)
            def _():
                swap_if(line_peer(j), False)

            @pl.when(jnp.logical_not(at_end) & (j == 2))
            def _():
                swap_all(line_peer, 1, False)

        sides(j, lambda line, side: halves_of(2 * line + y, stage_one))

        @pl.when(j >= 1)
        def _():
            mate_arrival(mate_source(j - 1))
            halves_of(mate_source(j - 1), stage_one)

        sides(j, lambda line, side: halves_of(2 * line + y, stage_two))

        @pl.when(j >= 1)
        def _():
            halves_of(mate_source(j - 1), stage_two)

        return carry

    lax.fori_loop(0, n_o, main_step, 0)
    last = mate_source(n_o - 1)

    def mate_homes(j, carry):
        halves_of(mate_source(j), stage_three)
        return carry

    def held_homes(j, carry):
        go_home(nth(j), True)
        return carry

    def drain_line(j, carry):
        line = nth(j)

        @pl.when(jnp.where(line < o, o + 1 < n_o, o > 0))
        def _():
            for p in range(2):
                cot_copy(0, p, 2 * line + y, mate, False).wait_send()

        return carry

    def drain_mate(j, carry):
        for p in range(2):
            cot_copy(2, p, 2 * nth(j) + y, mate, False).wait_send()
        return carry

    with jax.named_scope("drain_line"):
        for p in range(2):
            @pl.when(o + 1 < n_o)
            def _():
                cot_copy(0, p, row, row + 2, True).wait_send()

            @pl.when(o > 0)
            def _():
                cot_copy(1, p, row, row - 2, True).wait_send()

        lax.fori_loop(1, n_o, drain_line, 0)

    swap_all(line_peer, 1, True)
    lax.fori_loop(0, n_o, held_homes, 0)
    mate_arrival(last)
    with jax.named_scope("drain_mate"):
        for p in range(2):
            cot_copy(2, p, row, mate, True).wait_send()
        lax.fori_loop(1, n_o, drain_mate, 0)
    swap_all(mate_peer, 0, True)
    swap_all(mate_peer, 0, False)
    halves_of(last, stage_one)
    halves_of(last, stage_two)
    sides(n_o - 1, lambda line, side: go_home(line, False))
    first_shares(line_peer, 1)
    lax.fori_loop(0, n_o - 1, mate_homes, 0)
    second_shares(line_peer, 1)
    with jax.named_scope("weights"):
        lax.fori_loop(0, f_tiles, line_weights, 0)
    first_shares(mate_peer, 0)
    halves_of(last, stage_three)
    second_shares(mate_peer, 0)
    with jax.named_scope("weights"):
        lax.fori_loop(0, f_tiles, mate_weights, 0)

    late.wait()
    col_start = col * slice_width
    c_tile = tile(h_width, 256)
    model_width = width
    tiles = h_width // c_tile

    def lanes(value):
        total = value[:, 0:128]
        for k in range(1, c_tile // 128):
            total = total + value[:, k * 128 : (k + 1) * 128]
        return total

    def wide(value):
        return jnp.concatenate([value] * (c_tile // 128), axis=1)

    acc = jnp.zeros((tokens, 128), F32)
    for n in range(fold):
        j = (row + n) % fold
        for h in range(halves):
            for c in range(2):
                @pl.when(jnp.logical_not((col * fold + j == row) & (c == core)))
                def _():
                    arrived = fg.at[j, h, pl.ds(c * half, half)]
                    with jax.named_scope("wait_home"):
                        remote(
                            arrived, arrived, fs_send.at[0, 0], fs_recv.at[j, h, c],
                            row, 2 * x + 1 - core,
                        ).wait_recv()

            for t in range(tiles):
                at = j * feats + h * h_width + t * c_tile
                here = pl.ds(pl.multiple_of(col_start + at, c_tile), c_tile)
                there = pl.ds(pl.multiple_of(at, c_tile), c_tile)
                grad = fg[j, h, :, t * c_tile : (t + 1) * c_tile].astype(F32)
                product = grad * xin[:, here].astype(F32)
                acc = acc + lanes(product * gain[:, here])
                gains[:, there] = jnp.sum(product * wide(inv[...]), axis=0, keepdims=True)
    summed = jnp.broadcast_to(jnp.sum(acc, axis=1, keepdims=True), (tokens, 128))
    dots[...] = jnp.transpose(summed)[0:8, :]
    gains[:, slice_width:] = sq[...]

    dot_copies, gain_copies = [], []
    for k in range(1, n_col):
        dot_copies.append(
            remote(dots, dots_in.at[col], dot_send.at[k], dot_recv.at[k], row, (col + k) % n_col)
        )
    for k in range(1, n_row):
        gain_copies.append(
            remote(gains, gains_in.at[row], gain_send.at[k], gain_recv.at[k], (row + k) % n_row, col)
        )
    for copy in dot_copies + gain_copies:
        copy.start()
    dots_in[col] = dots[...]
    gains_in[row] = gains[...]
    with jax.named_scope("wait_gains"):
        for copy in gain_copies:
            copy.wait()
    all_gains = jnp.sum(gains_in[...], axis=0)
    grad_gain = all_gains[:, :slice_width] * (1.0 / math.sqrt(tokens * n_row))
    gains_out[...] = grad_gain
    squares = jnp.sum(grad_gain * grad_gain) + jnp.sum(all_gains[:, slice_width:])
    tot[...] = jnp.full(tot.shape, squares, F32)
    tot_copies = [
        remote(tot, tot_in.at[col], tot_send.at[k], tot_recv.at[k], row, (col + k) % n_col)
        for k in range(1, n_col)
    ]
    for copy in tot_copies:
        copy.start()
    tot_in[col] = tot[...]
    with jax.named_scope("wait_dots"):
        for copy in dot_copies:
            copy.wait()
    token_row = jnp.sum(dots_in[...], axis=0)[0:1, :]
    token_dot = jnp.transpose(jnp.broadcast_to(token_row, (128, tokens)))
    inv_rms = inv[...]
    inv_wide = wide(inv_rms)
    factor = wide(inv_rms * inv_rms * inv_rms * token_dot / model_width)
    for j in range(fold):
        for h in range(halves):
            for t in range(tiles):
                at = j * feats + h * h_width + t * c_tile
                here = pl.ds(pl.multiple_of(col_start + at, c_tile), c_tile)
                grad = fg[j, h, :, t * c_tile : (t + 1) * c_tile].astype(F32)
                value = (
                    resid[:, at : at + c_tile].astype(F32)
                    + inv_wide * gain[:, here] * grad
                    - xin[:, here].astype(F32) * factor
                )
                dout[:, at : at + c_tile] = value.astype(BF16)
    with jax.named_scope("wait_total"):
        for copy in tot_copies:
            copy.wait()
    total_out[...] = jnp.sum(tot_in[...], axis=0) / model_width

    def drain_row(k, carry):
        source = (row + k) % n_row
        for h in range(halves):
            pair_copy(source, h).wait_send()

            @pl.when(jnp.logical_not(at_home))
            def _():
                cross_copy(source, h).wait_send()

            @pl.when(at_home & jnp.logical_not((source == row) & (home_col == col)))
            def _():
                home_copy(source, h).wait_send()

        @pl.when(k >= 1)
        def _():
            core_share(source).wait_send()

            @pl.when(x == swap_x)
            def _():
                swap_copy(source).wait_send()

            @pl.when(x == swap_plane(source))
            def _():
                for i in range(1, n_x):
                    x_share(source, i).wait_send()

        return carry

    lax.fori_loop(0, n_row, drain_row, 0)


def store_kernel(*refs):
    count = len(refs) // 2
    sems = refs[-1]
    copies = [
        pltpu.make_async_copy(refs[i], refs[count + i], sems.at[i]) for i in range(count)
    ]
    for copy in copies:
        copy.start()
    for copy in copies:
        copy.wait()


def local(layer_input, gain, d_query, d_keyval, w_query, w_keyval, d_resid):
    n_row, n_col = lax.axis_size("row"), lax.axis_size("col")
    n_x, n_o, fold = n_col // 2, n_row // 2, n_row // n_col
    tokens, width = layer_input.shape
    q_cols, k_cols = d_query.shape[1], d_keyval.shape[1]
    feats, slice_width = width // n_row, width // n_col
    half = tokens // 2
    halves = 2 if feats // tile(feats, 256) % 2 == 0 else 1
    h_width = feats // halves
    dma = pltpu.SemaphoreType.DMA
    hbm = pl.BlockSpec(memory_space=pltpu.HBM)
    vmem = pl.BlockSpec(memory_space=pltpu.VMEM)
    shape = jax.ShapeDtypeStruct
    every = n_row * tokens
    pin = functools.partial(pltpu.with_memory_space_constraint, memory_space=pltpu.HBM)
    results = pl.pallas_call(
        functools.partial(step_kernel, n_row, n_col),
        out_shape=(
            pltpu.VMEM((tokens, slice_width), BF16),
            pltpu.VMEM((feats, q_cols), BF16),
            pltpu.VMEM((feats, k_cols), BF16),
            pltpu.VMEM((1, slice_width), F32),
            pltpu.VMEM((1, 128), F32),
        ),
        in_specs=[hbm] * 7,
        out_specs=[vmem] * 5,
        scratch_shapes=[
            pltpu.VMEM((every, q_cols), BF16),
            pltpu.VMEM((every, k_cols), BF16),
            pltpu.VMEM((tokens, width), BF16),
            pltpu.VMEM((tokens, width), BF16),
            pltpu.VMEM((every, feats), BF16),
            pltpu.VMEM((feats, q_cols), BF16),
            pltpu.VMEM((feats, k_cols), BF16),
            pltpu.VMEM((tokens, slice_width), BF16),
            pltpu.VMEM((halves, every, h_width), BF16),
            pltpu.VMEM((halves, n_row * half, h_width), BF16),
            pltpu.VMEM((halves, n_row * half, h_width), BF16),
            pltpu.VMEM((n_x, halves, n_row * half, h_width), BF16),
            pltpu.VMEM((fold, halves, tokens, h_width), BF16),
            pltpu.VMEM((1, width), F32),
            pltpu.VMEM((feats, q_cols), F32),
            pltpu.VMEM((feats, k_cols), F32),
            pltpu.VMEM((tokens, 128), F32),
            pltpu.VMEM((1, 128), F32),
            pltpu.VMEM((8, tokens), F32),
            pltpu.VMEM((n_col, 8, tokens), F32),
            pltpu.VMEM((1, slice_width + 128), F32),
            pltpu.VMEM((n_row, 1, slice_width + 128), F32),
            pltpu.VMEM((1, 128), F32),
            pltpu.VMEM((n_col, 1, 128), F32),
            dma((7,)),
            dma((n_o, 3, 2)),
            dma((n_row, 2)),
            dma((n_row,)),
            dma((n_row,)),
            dma((n_row, n_x)),
            dma((n_row,)),
            dma((n_row,)),
            dma((n_row, halves)),
            dma((n_row, halves)),
            dma((n_row, halves)),
            dma((n_x, n_row, halves)),
            dma((n_row, halves)),
            dma((fold, halves, 2)),
            dma((n_col,)),
            dma((n_col,)),
            dma((n_row,)),
            dma((n_row,)),
            dma((n_col,)),
            dma((n_col,)),
        ],
        compiler_params=pltpu.CompilerParams(
            collective_id=0, has_side_effects=True, vmem_limit_bytes=VMEM_LIMIT
        ),
        name="step",
    )(
        pin(layer_input), pin(gain.reshape(1, width)), pin(d_query), pin(d_keyval),
        pin(w_query), pin(w_keyval), pin(d_resid),
    )
    d_input, grad_wq, grad_wkv, grad_gain, total = pl.pallas_call(
        store_kernel,
        out_shape=tuple(shape(result.shape, result.dtype) for result in results),
        in_specs=[vmem] * 5,
        out_specs=[hbm] * 5,
        scratch_shapes=[dma((5,))],
        compiler_params=pltpu.CompilerParams(vmem_limit_bytes=1024 * 1024),
        name="store",
    )(*results)
    return (d_input, grad_wq, grad_wkv, grad_gain.reshape(slice_width), total[0, 0])


def solution(mesh):
    placed = (
        P("row", None),
        P(),
        P("row", "col"),
        P("row", "col"),
        P("row", "col"),
        P("row", "col"),
        P("row", "col"),
    )
    return jax.shard_map(
        local,
        mesh=mesh,
        in_specs=placed,
        out_specs=(P("row", "col"), P("row", "col"), P("row", "col"), P("col"), P()),
        check_vma=False,
    )
```

time: 143 us -> 129 us (0.902)
  Pallas kernels: 135 us -> 129 us
  local copies, waits for them, and re-layouts: 5.99 us -> 0 us
    unnamed x12 -> x0, local copies, waits for them, and re-layouts: 5.99 us -> none
    pallas_call x1 -> x2, Pallas kernels: 135 us -> 129 us  [the longest x1 127 us: local(): pl.pallas_call(functools.partial(step_kernel, n_row, n_col), out_shape=(p...]
where the time goes in v2:
time: 129 us
  Pallas kernels  129 us (100%)
    pallas_call x1, Pallas kernels, local(): pl.pallas_call(functools.partial(step_kernel, n_row, n_col), out_shape=(p...  127 us

profile of v2, /device:TPU:0, one launch (start us, length us, event | category | flops | bytes accessed | tf_op | source)
XLA Modules:
  0.0 129.3 jit_solution(17326442994878093100)
XLA Ops:
  0.6 126.6 %step.1 = (bf16[256,2048]{1,0:T(8,128)(2,1)S(1)}, bf16[1024,1024]{1,0:T(8,128)(2,1)S(1)}, bf16[1024,512]{1,0:T(8,128)(2,1)S(1)}, f32[1,2048]{1,0:T(1,128)S(1)}, f32[1,128]{1,0:T(1,128)S(1)}) custom-call(bf16[256,8192]{1,0:T(8,128)(2,1)} %x_hbm.1, f32[1,8192]{1,0:T(1,128)} %bitcast.4, bf16[256,1024]{1,0:T(8,128)(2,1)} %dq_hbm.1, bf16[256,512]{1,0:T(8,128)(2,1)} %dk_hbm.1, ...), custom_call_target="tpu_custom_call" | custom-call | tf_op jit(solution)/shard_map/step/pallas_call | solution.py:669
  127.3 2.1 %store.1 = (bf16[256,2048]{1,0:T(8,128)(2,1)}, bf16[1024,1024]{1,0:T(8,128)(2,1)}, bf16[1024,512]{1,0:T(8,128)(2,1)}, f32[1,2048]{1,0:T(1,128)}, f32[1,128]{1,0:T(1,128)}) custom-call(bf16[256,2048]{1,0:T(8,128)(2,1)S(1)} %get-tuple-element.15.refs_0_, bf16[1024,1024]{1,0:T(8,128)(2,1)S(1)} %get-tuple-element.16.refs_1_, ...), custom_call_target="tpu_custom_call" | custom-call | tf_op jit(solution)/shard_map/store/pallas_call | solution.py:734

commit v3 on v2

--- a/solution.py
+++ b/solution.py
@@ -24,10 +24,10 @@
     x_hbm, gain_hbm, dq_hbm, dk_hbm, wq_hbm, wk_hbm, resid_hbm,
     dout, gq, gk, gains_out, total_out,
     cotq, cotk, xin, normed, ncols, wq, wk, resid, pfull, precv, csend, xrecv, fg,
-    gain, acc_q, acc_k, inv, sq, dots, dots_in, gains, gains_in, tot, tot_in,
+    gain, acc_q, acc_k, inv, sq, dots, dots_in, gains, gains_in, tot, tot_in, sq_in,
     load_sem, cot_send, cot_recv, swap_send, swap_recv, xs_send,
     cs_send, cs_recv, pe_send, pe_recv, xr_send, xr_recv, fs_send, fs_recv,
-    dot_send, dot_recv, gain_send, gain_recv, tot_send, tot_recv,
+    dot_send, dot_recv, gain_send, gain_recv, tot_send, tot_recv, sq_send, sq_recv, credit,
 ):
     row, col = lax.axis_index("row"), lax.axis_index("col")
     tokens, width = xin.shape
@@ -209,11 +209,16 @@
             share_second(peer(k))
             return carry
 
+        lax.fori_loop(start, n_o, one, 0)
+
+    def core_shares(peer, start, direct):
         def wait(k, carry):
-            core_share(peer(k)).wait_recv()
+            @pl.when((x == swap_plane(peer(k))) == direct)
+            def _():
+                core_share(peer(k)).wait_recv()
+
             return carry
 
-        lax.fori_loop(start, n_o, one, 0)
         with jax.named_scope("wait_share"):
             lax.fori_loop(start, n_o, wait, 0)
 
@@ -322,11 +327,11 @@
     groups = []
     for held, kept, total in ((cotq, gq, acc_q), (cotk, gk, acc_k)):
         groups.append((held, kept, total, tile(held.shape[1], 512)))
-    line_rows = n_o * tokens
-
-    def products(i, line, action):
+    group_lines = n_o // n_x
+
+    def products(i, first, count, action):
         fs = pl.ds(pl.multiple_of(i * f_tile, f_tile), f_tile)
-        rows = pl.ds(pl.multiple_of(line * line_rows, line_rows), line_rows)
+        rows = pl.ds(pl.multiple_of(first * tokens, tokens), count * tokens)
         for held, kept, total, k_tile in groups:
             for k in range(held.shape[1] // k_tile):
                 ks = pl.ds(k * k_tile, k_tile)
@@ -339,20 +344,29 @@
         def keep_sum(value, kept, total, fs, ks, k_tile):
             total[fs, ks] = value
 
-        products(i, y, keep_sum)
-        return carry
-
-    def mate_weights(i, carry):
-        def finish(value, kept, total, fs, ks, k_tile):
-            value = ((value + total[fs, ks]) * weight_scale).astype(BF16)
-            kept[fs, ks] = value
-            value = value.astype(F32)
-            value = jnp.sum(value * value, axis=0, keepdims=True)
-            for at in range(0, k_tile, 128):
-                sq[...] += value[:, at : at + 128]
-
-        products(i, 1 - y, finish)
-        return carry
+        products(i, y * n_o, n_o, keep_sum)
+        return carry
+
+    def mate_weights(group, last_one):
+        first = (1 - y) * n_o + group * group_lines
+
+        def one(i, carry):
+            def add(value, kept, total, fs, ks, k_tile):
+                total[fs, ks] += value
+
+            def finish(value, kept, total, fs, ks, k_tile):
+                value = ((value + total[fs, ks]) * weight_scale).astype(BF16)
+                kept[fs, ks] = value
+                value = value.astype(F32)
+                value = jnp.sum(value * value, axis=0, keepdims=True)
+                for at in range(0, k_tile, 128):
+                    sq[...] += value[:, at : at + 128]
+
+            products(i, first, group_lines, finish if last_one else add)
+            return carry
+
+        with jax.named_scope("weights"):
+            lax.fori_loop(0, f_tiles, one, 0)
 
     f_tiles = feats // f_tile
     sq[...] = jnp.zeros_like(sq)
@@ -370,12 +384,29 @@
 
         lax.fori_loop(0, halves, one, 0)
 
+    at_end = (o == 0) | (o == n_o - 1)
+    inward = jnp.where(o == 0, row + 2, row - 2)
+    inward_way = jnp.where(o == 0, 1, 0)
+
+    def by_mate(line):
+        low = (o == 1) & (line == 0)
+        high = (o == n_o - 2) & (line == n_o - 1)
+        return jnp.logical_not(low | high)
+
     def mate_arrival(source):
         for p in range(2):
             with jax.named_scope("wait_mate"):
                 cot_copy(0, p, source, mate, False).wait_recv()
 
-    at_end = (o == 0) | (o == n_o - 1)
+            @pl.when(at_end & (source == mate))
+            def _():
+                relay_copy(p).start()
+
+    def relay_copy(p):
+        held = pieces[p][1].at[block(mate)]
+        return remote(
+            held, held, cot_send.at[o, inward_way, p], cot_recv.at[mate, p], inward, col
+        )
 
     def swap_if(target, end):
         line = target // 2
@@ -415,7 +446,9 @@
             def _():
                 cot_copy(0, p, source, to_row, False).start()
 
-            cot_copy(2, p, source, mate, False).start()
+            @pl.when(by_mate(line))
+            def _():
+                cot_copy(2, p, source, mate, False).start()
 
     def go_home(line, held):
         late_one = ((line == 0) | (line == n_o - 1)) & jnp.logical_not(at_end)
@@ -475,8 +508,11 @@
         return carry
 
     def drain_mate(j, carry):
-        for p in range(2):
-            cot_copy(2, p, 2 * nth(j) + y, mate, False).wait_send()
+        @pl.when(by_mate(nth(j)))
+        def _():
+            for p in range(2):
+                cot_copy(2, p, 2 * nth(j) + y, mate, False).wait_send()
+
         return carry
 
     with jax.named_scope("drain_line"):
@@ -491,28 +527,71 @@
 
         lax.fori_loop(1, n_o, drain_line, 0)
 
-    swap_all(line_peer, 1, True)
-    lax.fori_loop(0, n_o, held_homes, 0)
+        @pl.when(at_end)
+        def _():
+            for p in range(2):
+                relay_copy(p).wait_send()
+
+    own_end = jnp.where(o == 0, 0, 1)
+
+    def tell(peer, start, base):
+        def one(k, carry):
+            pl.semaphore_signal(
+                credit.at[base + own_end], inc=1,
+                device_id=(peer(k), col), device_id_type=MESH,
+            )
+            return carry
+
+        @pl.when(at_end)
+        def _():
+            lax.fori_loop(start, n_o, one, 0)
+
+    def heed(base):
+        for i in range(2):
+            @pl.when((base == 2) | (o != i * (n_o - 1)))
+            def _():
+                pl.semaphore_wait(credit.at[base + i], 1)
+
+    tell(line_peer, 1, 0)
+
+    @pl.when(at_end)
+    def _():
+        swap_all(mate_peer, 0, False)
+
     mate_arrival(last)
+    tell(mate_peer, 0, 2)
     with jax.named_scope("drain_mate"):
         for p in range(2):
             cot_copy(2, p, row, mate, True).wait_send()
         lax.fori_loop(1, n_o, drain_mate, 0)
-    swap_all(mate_peer, 0, True)
-    swap_all(mate_peer, 0, False)
+
+    @pl.when(jnp.logical_not(at_end))
+    def _():
+        swap_all(mate_peer, 0, False)
+
     halves_of(last, stage_one)
     halves_of(last, stage_two)
+    with jax.named_scope("heed_line"):
+        heed(0)
+    swap_all(line_peer, 1, True)
+    lax.fori_loop(0, n_o, held_homes, 0)
     sides(n_o - 1, lambda line, side: go_home(line, False))
+    with jax.named_scope("heed_mate"):
+        heed(2)
+    swap_all(mate_peer, 0, True)
     first_shares(line_peer, 1)
     lax.fori_loop(0, n_o - 1, mate_homes, 0)
+    halves_of(last, stage_three)
     second_shares(line_peer, 1)
+    first_shares(mate_peer, 0)
+    core_shares(line_peer, 1, True)
+    core_shares(line_peer, 1, False)
     with jax.named_scope("weights"):
         lax.fori_loop(0, f_tiles, line_weights, 0)
-    first_shares(mate_peer, 0)
-    halves_of(last, stage_three)
+    core_shares(mate_peer, 0, True)
+    mate_weights((x + n_x // 2) % n_x, n_x == 1)
     second_shares(mate_peer, 0)
-    with jax.named_scope("weights"):
-        lax.fori_loop(0, f_tiles, mate_weights, 0)
+    core_shares(mate_peer, 0, False)
 
     late.wait()
     col_start = col * slice_width
@@ -553,7 +632,6 @@
                 gains[:, there] = jnp.sum(product * wide(inv[...]), axis=0, keepdims=True)
     summed = jnp.broadcast_to(jnp.sum(acc, axis=1, keepdims=True), (tokens, 128))
     dots[...] = jnp.transpose(summed)[0:8, :]
-    gains[:, slice_width:] = sq[...]
 
     dot_copies, gain_copies = [], []
     for k in range(1, n_col):
@@ -566,16 +644,27 @@
         )
     for copy in dot_copies + gain_copies:
         copy.start()
+    for i in range(1, n_x):
+        mate_weights((x + n_x // 2 + i) % n_x, i == n_x - 1)
+    square_copies = [
+        remote(sq, sq_in.at[row], sq_send.at[k], sq_recv.at[k], (row + k) % n_row, col)
+        for k in range(1, n_row)
+    ]
+    for copy in square_copies:
+        copy.start()
+    sq_in[row] = sq[...]
     dots_in[col] = dots[...]
     gains_in[row] = gains[...]
     with jax.named_scope("wait_gains"):
         for copy in gain_copies:
             copy.wait()
-    all_gains = jnp.sum(gains_in[...], axis=0)
-    grad_gain = all_gains[:, :slice_width] * (1.0 / math.sqrt(tokens * n_row))
+    grad_gain = jnp.sum(gains_in[...], axis=0) * (1.0 / math.sqrt(tokens * n_row))
     gains_out[...] = grad_gain
-    squares = jnp.sum(grad_gain * grad_gain) + jnp.sum(all_gains[:, slice_width:])
-    tot[...] = jnp.full(tot.shape, squares, F32)
+    gain_squares = jnp.sum(grad_gain * grad_gain)
+    with jax.named_scope("wait_squares"):
+        for copy in square_copies:
+            copy.wait()
+    tot[...] = jnp.full(tot.shape, gain_squares + jnp.sum(sq_in[...]), F32)
     tot_copies = [
         remote(tot, tot_in.at[col], tot_send.at[k], tot_recv.at[k], row, (col + k) % n_col)
         for k in range(1, n_col)
@@ -698,10 +787,11 @@
             pltpu.VMEM((1, 128), F32),
             pltpu.VMEM((8, tokens), F32),
             pltpu.VMEM((n_col, 8, tokens), F32),
-            pltpu.VMEM((1, slice_width + 128), F32),
-            pltpu.VMEM((n_row, 1, slice_width + 128), F32),
+            pltpu.VMEM((1, slice_width), F32),
+            pltpu.VMEM((n_row, 1, slice_width), F32),
             pltpu.VMEM((1, 128), F32),
             pltpu.VMEM((n_col, 1, 128), F32),
+            pltpu.VMEM((n_row, 1, 128), F32),
             dma((7,)),
             dma((n_o, 3, 2)),
             dma((n_row, 2)),
@@ -722,6 +812,9 @@
             dma((n_row,)),
             dma((n_col,)),
             dma((n_col,)),
+            dma((n_row,)),
+            dma((n_row,)),
+            pltpu.SemaphoreType.REGULAR((4,)),
         ],
         compiler_params=pltpu.CompilerParams(
             collective_id=0, has_side_effects=True, vmem_limit_bytes=VMEM_LIMIT

time: 129 us -> 125 us (0.969)
  Pallas kernels: 129 us -> 124 us
    pallas_call x1, Pallas kernels: 127 us -> 122 us  [local(): pl.pallas_call(functools.partial(step_kernel, n_row, n_col), out_shape=(p...]
where the time goes in v3:
time: 125 us; the launch traced here: 124 us
  Pallas kernels  124 us (99%)
    pallas_call x1, Pallas kernels, local(): pl.pallas_call(functools.partial(step_kernel, n_row, n_col), out_shape=(p...  122 us

profile of v3, /device:TPU:0, one launch (start us, length us, event | category | flops | bytes accessed | tf_op | source)
XLA Modules:
  0.0 124.5 jit_solution(10100275198205167500)
XLA Ops:
  0.6 121.8 %step.1 = (bf16[256,2048]{1,0:T(8,128)(2,1)S(1)}, bf16[1024,1024]{1,0:T(8,128)(2,1)S(1)}, bf16[1024,512]{1,0:T(8,128)(2,1)S(1)}, f32[1,2048]{1,0:T(1,128)S(1)}, f32[1,128]{1,0:T(1,128)S(1)}) custom-call(bf16[256,8192]{1,0:T(8,128)(2,1)} %x_hbm.1, f32[1,8192]{1,0:T(1,128)} %bitcast.4, bf16[256,1024]{1,0:T(8,128)(2,1)} %dq_hbm.1, bf16[256,512]{1,0:T(8,128)(2,1)} %dk_hbm.1, ...), custom_call_target="tpu_custom_call" | custom-call | tf_op jit(solution)/shard_map/step/pallas_call | solution.py:758
  122.4 2.1 %store.1 = (bf16[256,2048]{1,0:T(8,128)(2,1)}, bf16[1024,1024]{1,0:T(8,128)(2,1)}, bf16[1024,512]{1,0:T(8,128)(2,1)}, f32[1,2048]{1,0:T(1,128)}, f32[1,128]{1,0:T(1,128)}) custom-call(bf16[256,2048]{1,0:T(8,128)(2,1)S(1)} %get-tuple-element.15.refs_0_, bf16[1024,1024]{1,0:T(8,128)(2,1)S(1)} %get-tuple-element.16.refs_1_, ...), custom_call_target="tpu_custom_call" | custom-call | tf_op jit(solution)/shard_map/store/pallas_call | solution.py:827

commit v4 on v3

--- a/solution.py
+++ b/solution.py
@@ -655,6 +655,36 @@
     sq_in[row] = sq[...]
     dots_in[col] = dots[...]
     gains_in[row] = gains[...]
+    def drain_row(k, carry):
+        source = (row + k) % n_row
+        for h in range(halves):
+            pair_copy(source, h).wait_send()
+
+            @pl.when(jnp.logical_not(at_home))
+            def _():
+                cross_copy(source, h).wait_send()
+
+            @pl.when(at_home & jnp.logical_not((source == row) & (home_col == col)))
+            def _():
+                home_copy(source, h).wait_send()
+
+        @pl.when(k >= 1)
+        def _():
+            core_share(source).wait_send()
+
+            @pl.when(x == swap_x)
+            def _():
+                swap_copy(source).wait_send()
+
+            @pl.when(x == swap_plane(source))
+            def _():
+                for i in range(1, n_x):
+                    x_share(source, i).wait_send()
+
+        return carry
+
+    lax.fori_loop(0, n_row, drain_row, 0)
+
     with jax.named_scope("wait_gains"):
         for copy in gain_copies:
             copy.wait()
@@ -696,36 +726,6 @@
         for copy in tot_copies:
             copy.wait()
     total_out[...] = jnp.sum(tot_in[...], axis=0) / model_width
-
-    def drain_row(k, carry):
-        source = (row + k) % n_row
-        for h in range(halves):
-            pair_copy(source, h).wait_send()
-
-            @pl.when(jnp.logical_not(at_home))
-            def _():
-                cross_copy(source, h).wait_send()
-
-            @pl.when(at_home & jnp.logical_not((source == row) & (home_col == col)))
-            def _():
-                home_copy(source, h).wait_send()
-
-        @pl.when(k >= 1)
-        def _():
-            core_share(source).wait_send()
-
-            @pl.when(x == swap_x)
-            def _():
-                swap_copy(source).wait_send()
-
-            @pl.when(x == swap_plane(source))
-            def _():
-                for i in range(1, n_x):
-                    x_share(source, i).wait_send()
-
-        return carry
-
-    lax.fori_loop(0, n_row, drain_row, 0)
 
 
 def store_kernel(*refs):

time: 125 us -> 124 us (level)
  no operation moved by 1% of the time
where the time goes in v4:
time: 124 us
  Pallas kernels  124 us (100%)
    pallas_call x1, Pallas kernels, local(): pl.pallas_call(functools.partial(step_kernel, n_row, n_col), out_shape=(p...  121 us

profile of v4, /device:TPU:0, one launch (start us, length us, event | category | flops | bytes accessed | tf_op | source)
XLA Modules:
  0.0 124.1 jit_solution(8253335568270713599)
XLA Ops:
  0.6 121.5 %step.1 = (bf16[256,2048]{1,0:T(8,128)(2,1)S(1)}, bf16[1024,1024]{1,0:T(8,128)(2,1)S(1)}, bf16[1024,512]{1,0:T(8,128)(2,1)S(1)}, f32[1,2048]{1,0:T(1,128)S(1)}, f32[1,128]{1,0:T(1,128)S(1)}) custom-call(bf16[256,8192]{1,0:T(8,128)(2,1)} %x_hbm.1, f32[1,8192]{1,0:T(1,128)} %bitcast.4, bf16[256,1024]{1,0:T(8,128)(2,1)} %dq_hbm.1, bf16[256,512]{1,0:T(8,128)(2,1)} %dk_hbm.1, ...), custom_call_target="tpu_custom_call" | custom-call | tf_op jit(solution)/shard_map/step/pallas_call | solution.py:758
  122.1 2.1 %store.1 = (bf16[256,2048]{1,0:T(8,128)(2,1)}, bf16[1024,1024]{1,0:T(8,128)(2,1)}, bf16[1024,512]{1,0:T(8,128)(2,1)}, f32[1,2048]{1,0:T(1,128)}, f32[1,128]{1,0:T(1,128)}) custom-call(bf16[256,2048]{1,0:T(8,128)(2,1)S(1)} %get-tuple-element.15.refs_0_, bf16[1024,1024]{1,0:T(8,128)(2,1)S(1)} %get-tuple-element.16.refs_1_, ...), custom_call_target="tpu_custom_call" | custom-call | tf_op jit(solution)/shard_map/store/pallas_call | solution.py:827
